TPU v7x, 32 devices: a whole 2x2x4 slice. The times are simulated.
32 devices in a mesh: beam: 2 (over x), tm: 16 (over z, y, core).
Axes of the slice: x: 2, y: 2, z: 4, core: 2. Of those that a mesh axis runs over, the one named last changes fastest.
Arguments:
- voltage: bfloat16 [2, 2, 2097152], P(None, None, ('beam', 'tm')), parts along dimension 2, may hold values from -11 to 11
- delays: int32 [64, 2048], replicated, may hold values from 0 to 96, as said below
- chan_mask: int32 [4096], P('beam'), parts along dimension 0, may hold values 0 or 1
Outputs:
- zscore: float32 [64, 1024], P(None, ('beam', 'tm')), parts along dimension 1
- trial_stats: float32 [3, 128], P(None, 'beam'), parts along dimension 1
There are 2 independent parts, one for each index of `beam`. A program takes and returns all parts, laid end to end along the dimension named above; an argument that names none is the same for every part. Nothing has to cross between parts.
Inputs may be any that keep to these rules, and one draw needn't show every extreme that they name: For each trial the delays never rise from one channel to the next; the last channel's delays are 0, and the first channel's delay of some trial is 96.
All inputs are finite; a program needn't handle non-finite values.
Results may differ from a plain program's by a relative error of at most 0.002.
Values may be sent and summed in bfloat16 or wider, within the bound.
No kernel may reach another device: no remote copies, remote signals or barrier semaphores. Data moves between devices by JAX's collectives and lax.ppermute only.
A program may use at most 64 MiB of HBM per device.

v0:
```python
import math

import jax
import jax.numpy as jnp
from jax import lax
from jax.sharding import PartitionSpec as P

NCHAN = 2048
TAPS = 16
DSPAN = 3


highest = lax.Precision.HIGHEST
shift_group = 8


def passed_along(value, axis, steps):
    count = lax.axis_size(axis)
    first, last = (max(0, -steps), min(count, count - steps))
    return lax.ppermute(value, axis, [(source, source + steps) for source in range(first, last)])


def prototype(tap_count, chan_count):
    length = tap_count * chan_count
    position = jnp.arange(length, dtype=jnp.float32)
    centred = (position - (length - 1) / 2.0) / chan_count
    window = 0.54 - 0.46 * jnp.cos(2.0 * jnp.pi * position / (length - 1))
    shaped = jnp.sinc(centred) * window
    shaped = shaped * jnp.sqrt(chan_count / jnp.sum(shaped * shaped))
    return shaped.reshape(tap_count, chan_count)


def phase_table(row_count, col_count, period):
    product = (
        jnp.arange(row_count, dtype=jnp.int32)[:, None]
        * jnp.arange(col_count, dtype=jnp.int32)[None, :]
        % period
    )
    angles = product.astype(jnp.float32) * (-2.0 * jnp.pi / period)
    return (jnp.cos(angles), jnp.sin(angles))


def spectral_power(weighted, chan_count):
    frame_count = weighted.shape[2]
    low_count = chan_count // 128
    split_up = weighted.reshape(2, 2, frame_count, low_count, 128)
    real_part = split_up[:, 0]
    imag_part = split_up[:, 1]
    cos_first, sin_first = phase_table(low_count, low_count, low_count)
    section_real = jnp.einsum(
        "pfmn,mk->pfkn", real_part, cos_first, precision=highest
    ) - jnp.einsum("pfmn,mk->pfkn", imag_part, sin_first, precision=highest)
    section_imag = jnp.einsum(
        "pfmn,mk->pfkn", real_part, sin_first, precision=highest
    ) + jnp.einsum("pfmn,mk->pfkn", imag_part, cos_first, precision=highest)
    cos_twist, sin_twist = phase_table(low_count, 128, chan_count)
    twist_real = section_real * cos_twist - section_imag * sin_twist
    twist_imag = section_real * sin_twist + section_imag * cos_twist
    cos_second, sin_second = phase_table(128, 128, 128)
    scale_factor = 1.0 / math.sqrt(chan_count)
    cos_second = cos_second * scale_factor
    sin_second = sin_second * scale_factor
    final_real = jnp.einsum(
        "pfkn,nj->pfkj", twist_real, cos_second, precision=highest
    ) - jnp.einsum("pfkn,nj->pfkj", twist_imag, sin_second, precision=highest)
    final_imag = jnp.einsum(
        "pfkn,nj->pfkj", twist_real, sin_second, precision=highest
    ) + jnp.einsum("pfkn,nj->pfkj", twist_imag, cos_second, precision=highest)
    energy = jnp.sum(final_real * final_real + final_imag * final_imag, axis=0)
    return jnp.transpose(energy, (2, 1, 0)).reshape(chan_count, frame_count).astype(jnp.bfloat16)


def dedisperse(padded, delays, out_width, max_delay):
    chan_count = padded.shape[0]
    group_count = (max_delay + shift_group) // shift_group
    needed = out_width + group_count * shift_group
    padded = jnp.concatenate(
        [padded, jnp.zeros((chan_count, needed - padded.shape[1]), padded.dtype)], axis=1
    )
    within = jnp.arange(shift_group, dtype=jnp.int32)

    def add_group(group_index, running):
        base = (group_index * shift_group).astype(jnp.int32)
        window = lax.dynamic_slice_in_dim(padded, base, out_width + shift_group - 1, 1)
        stacked = jnp.stack(
            [window[:, offset : offset + out_width] for offset in range(shift_group)]
        )
        targets = base + within
        selector = (delays[:, None, :] == targets[None, :, None]).astype(jnp.bfloat16)
        return running + jnp.einsum(
            "dsk,skt->dt", selector, stacked, preferred_element_type=jnp.float32
        )

    zero_sums = jnp.zeros((delays.shape[0], out_width), jnp.float32)
    return lax.fori_loop(0, group_count, add_group, zero_sums)


def per_device(voltage, delays, chan_mask):
    frame_count = voltage.shape[2] // NCHAN
    framed = voltage.reshape(2, 2, frame_count, NCHAN)
    history = passed_along(framed[:, :, frame_count - (TAPS - 1) :], "tm", 1)
    extended = jnp.concatenate([history, framed], axis=2)
    coeffs = prototype(TAPS, NCHAN)
    weighted = jnp.zeros((2, 2, frame_count, NCHAN), jnp.float32)
    for tap_index in range(TAPS):
        weighted = weighted + coeffs[tap_index] * extended[
            :, :, tap_index : tap_index + frame_count
        ].astype(jnp.float32)
    detected = spectral_power(weighted, NCHAN)
    masked = detected * chan_mask.astype(jnp.bfloat16)[:, None]
    max_delay = DSPAN * frame_count
    gathered = masked
    held_shards = 1
    while held_shards < DSPAN + 1:
        fetched = passed_along(gathered, "tm", -held_shards)
        gathered = jnp.concatenate([gathered, fetched], axis=1)
        held_shards = held_shards * 2
    series = dedisperse(gathered, delays, frame_count, max_delay)
    local_frames = series.shape[1]
    total_frames = local_frames * lax.axis_size("tm")
    totals = lax.psum(jnp.sum(series, axis=1), "tm")
    peak_value = lax.pmax(jnp.max(series, axis=1), "tm")
    average = totals / total_frames
    centred = series - average[:, None]
    variance = lax.psum(jnp.sum(centred * centred, axis=1), "tm") / total_frames
    deviation = jnp.sqrt(variance + 1e-05)
    zscore = centred / deviation[:, None]
    live_count = jnp.maximum(jnp.sum(chan_mask).astype(jnp.float32), 1.0)
    trial_stats = jnp.stack(
        [average / live_count, deviation / live_count, (peak_value - average) / deviation]
    )
    return (zscore, trial_stats)


def solution(mesh):
    in_specs = (P(None, None, ("beam", "tm")), P(), P("beam"))
    out_specs = (P(None, ("beam", "tm")), P(None, "beam"))
    return jax.shard_map(
        per_device, mesh=mesh, in_specs=in_specs, out_specs=out_specs, check_vma=False
    )
```

profile of v0, /device:TPU:0, one launch (start us, length us, event | category | flops | bytes accessed | tf_op | source)
XLA Modules:
  0.0 158.4 jit_solution(6258443623836400769)
XLA Ops:
  0.6 1.4 reshape.106
  2.2 2.4 %collective-permute-start = (bf16[2,2,15,2048]{3,2,0,1:T(8,128)(2,1)S(1)}, bf16[2,2,15,2048]{3,2,0,1:T(8,128)(2,1)S(1)}, u32[]{:S(2)}, u32[]{:S(2)}) collective-permute-start(bf16[2,2,15,2048]{3,2,0,1:T(8,128)(2,1)S(1)} %slice.217), channel_id=1, source_target_pairs={{0,1},{1,2},{2,3},{3,4},{4,5},{5,6},{6,7},{7,8},{8,9},{9,10},{10,1... | collective-permute-start | bytes 737288 | tf_op jit(solution)/shard_map/ppermute | solution.py:20
  4.6 1.2 multiply_reduce_fusion
  7.9 2.6 %multiply_add_fusion = f32[2,2,32,2048]{3,2,0,1:T(8,128)S(1)} fusion(bf16[2,2,32,2048]{3,2,0,1:T(8,128)(2,1)S(1)} %copy.12, bf16[2,2,15,2048]{3,2,0,1:T(8,128)(2,1)S(1)} %collective-permute-done, f32[2048]{0:T(1024)S(1)} %get-tuple-element.133, f32[2048]{0:T(1024)S(1)} %get-tuple-element.134, f32[2048]{0:T(1024)S(1)} %get-tuple-element.135, ...), kind=kLoop, calls=%fused_computation.61 | loop fusion | flops 24117248 | bytes 1949696 | tf_op jit(solution)/shard_map/add | solution.py:106
  17.4 1.3 collective-permute-start.1
  18.7 4.6 %collective-permute-done.1 = bf16[2048,32]{1,0:T(8,128)(2,1)S(1)} collective-permute-done((bf16[2048,32]{1,0:T(8,128)(2,1)S(1)}, bf16[2048,32]{1,0:T(8,128)(2,1)S(1)}, u32[]{:S(2)}, u32[]{:S(2)}) %collective-permute-start.1) | collective-permute-done | bytes 131104 | tf_op jit(solution)/shard_map/ppermute | solution.py:20
  23.6 1.5 collective-permute-start.2
  25.8 18.1 %collective-permute-done.2 = bf16[2048,64]{1,0:T(8,128)(2,1)S(1)} collective-permute-done((bf16[2048,64]{1,0:T(8,128)(2,1)S(1)}, bf16[2048,64]{1,0:T(8,128)(2,1)S(1)}, u32[]{:S(2)}, u32[]{:S(2)}) %collective-permute-start.2) | collective-permute-done | bytes 262176 | tf_op jit(solution)/shard_map/ppermute | solution.py:20
  43.9 0.9 maximum_maximum_fusion
  45.8 17.2 %while.14 = (s32[]{:T(128)}, f32[64,32]{0,1:T(8,128)S(1)}, s32[64,2048]{1,0:T(8,128)S(1)}, bf16[2048,136]{0,1:T(8,128)(2,1)S(1)}, s32[]{:T(128)}, /*index=5*/s32...) while((s32[]{:T(128)}, f32[64,32]{0,1:T(8,128)S(1)}, ...), condition=%wide.region_3.4_spmd.clone, body=%wide.region_2.3_spmd.clone.sunk | while | flops 68161560 | bytes 3686781 | solution.py:95
  46.2 0.9 fusion.178
  47.6 0.9 fusion.178
  48.9 0.9 fusion.178
  50.2 0.9 fusion.178
  51.6 0.9 fusion.178
  52.9 0.9 fusion.178
  54.2 0.9 fusion.178
  56.9 0.9 fusion.178
  58.2 0.9 fusion.178
  60.9 0.9 fusion.178
  62.2 0.9 fusion.178
  63.1 35.0 %psum.14 = f32[64]{0:T(128)S(1)} all-reduce(f32[64]{0:T(128)S(1)} %get-tuple-element.123), channel_id=1, replica_groups=mesh['beam'=2,'tm'=16] {'tm'}, use_global_device_ids=true, to_apply=%region_5.6 | all-reduce | flops 64 | bytes 512 | tf_op jit(solution)/shard_map/psum | solution.py:121
  98.2 29.5 %psum.15 = f32[64]{0:T(128)S(1)} all-reduce(f32[64]{0:T(128)S(1)} %multiply_reduce_fusion.1), channel_id=1, replica_groups=mesh['beam'=2,'tm'=16] {'tm'}, use_global_device_ids=true, to_apply=%region_7.8 | all-reduce | flops 64 | bytes 512 | tf_op jit(solution)/shard_map/psum | solution.py:125
  127.7 29.5 %pmax.7 = f32[64]{0:T(128)S(1)} all-reduce(f32[64]{0:T(128)S(1)} %get-tuple-element.122), channel_id=1, replica_groups=mesh['beam'=2,'tm'=16] {'tm'}, use_global_device_ids=true, to_apply=%region_10.11 | all-reduce | flops 64 | bytes 512 | tf_op jit(solution)/shard_map/pmax | solution.py:122
  (152 shorter events, 16.6 us)
Async XLA Ops:
  2.0 5.2 %copy-start = (s32[2048]{0:T(1024)S(1)}, s32[2048]{0:T(1024)}, u32[]{:S(2)}) copy-start(s32[2048]{0:T(1024)} %param.7) | copy-start | bytes 24580
  2.2 5.8 %collective-permute-start = (bf16[2,2,15,2048]{3,2,0,1:T(8,128)(2,1)S(1)}, bf16[2,2,15,2048]{3,2,0,1:T(8,128)(2,1)S(1)}, u32[]{:S(2)}, u32[]{:S(2)}) collective-permute-start(bf16[2,2,15,2048]{3,2,0,1:T(8,128)(2,1)S(1)} %slice.217), channel_id=1, source_target_pairs={{0,1},{1,2},{2,3},{3,4},{4,5},{5,6},{6,7},{7,8},{8,9},{9,10},{10,1... | collective-permute-start | bytes 737288 | tf_op jit(solution)/shard_map/ppermute | solution.py:20
  17.4 5.9 %collective-permute-start.1 = (bf16[2048,32]{1,0:T(8,128)(2,1)S(1)}, bf16[2048,32]{1,0:T(8,128)(2,1)S(1)}, u32[]{:S(2)}, u32[]{:S(2)}) collective-permute-start(bf16[2048,32]{1,0:T(8,128)(2,1)S(1)} %bitcast_multiply_fusion), channel_id=1, source_target_pairs={{1,0},{2,1},{3,2},{4,3},{5,4},{6,5},{7,6},{8,7},{9,8},{10,9},{11,1... | collective-permute-start | bytes 393224 | tf_op jit(solution)/shard_map/ppermute | solution.py:20
  23.6 20.3 %collective-permute-start.2 = (bf16[2048,64]{1,0:T(8,128)(2,1)S(1)}, bf16[2048,64]{1,0:T(8,128)(2,1)S(1)}, u32[]{:S(2)}, u32[]{:S(2)}) collective-permute-start(bf16[2048,64]{1,0:T(8,128)(2,1)S(1)} %pad_maximum_fusion.1), channel_id=1, source_target_pairs={{2,0},{3,1},{4,2},{5,3},{6,4},{7,5},{8,6},{9,7},{10,8},{11,9},{12,... | collective-permute-start | bytes 786440 | tf_op jit(solution)/shard_map/ppermute | solution.py:20
  44.8 1.0 copy-start.1
where the time goes:
time: 159 us; the launch traced here: 158 us
  blocking collectives  94 us (59%)
  waiting for transfers between devices  22.7 us (14%)
  matrix products  17.3 us (11%)
  other arithmetic  8.09 us (5%)
  local copies, waits for them, and re-layouts  7.21 us (5%)
  starting transfers between devices  5.18 us (3%)
  between operations  2.24 us (1%)
  loops' own time  1.66 us (1%)
    psum x1, blocking collectives, per_device(): totals = lax.psum(jnp.sum(series, axis=1), 'tm')  35 us
    psum x1, blocking collectives, per_device(): variance = lax.psum(jnp.sum(centred * centred, axis=1), 'tm') / total_frames  29.5 us
    pmax x1, blocking collectives, per_device(): peak_value = lax.pmax(jnp.max(series, axis=1), 'tm')  29.5 us
    ppermute x3, waiting for transfers between devices, passed_along(): lax.ppermute(value, axis, [(source, source + steps) for source in range(f...  22.7 us
    dot_general x13, matrix products, add_group(): jnp.einsum('dsk,skt->dt', selector, stacked, preferred_element_type=jnp.f...  11.5 us
    ppermute x3, starting transfers between devices, passed_along(): lax.ppermute(value, axis, [(source, source + steps) for source in range(f...  5.18 us
    while x91, local copies, waits for them, and re-layouts  3.45 us
  transfers between devices with their start and end apart: 3, of which 2 were waited for; matrix products, arithmetic and copies ran while one was open for 2% of the time, Pallas kernels for 0%

commit v1 on v0

--- a/solution.py
+++ b/solution.py
@@ -118,11 +118,18 @@
     series = dedisperse(gathered, delays, frame_count, max_delay)
     local_frames = series.shape[1]
     total_frames = local_frames * lax.axis_size("tm")
-    totals = lax.psum(jnp.sum(series, axis=1), "tm")
-    peak_value = lax.pmax(jnp.max(series, axis=1), "tm")
-    average = totals / total_frames
+    local_sum = jnp.sum(series, axis=1)
+    local_centred = series - (local_sum / local_frames)[:, None]
+    packed = jnp.stack(
+        [local_sum, jnp.max(series, axis=1), jnp.sum(local_centred * local_centred, axis=1)]
+    )
+    count = lax.axis_size("tm")
+    shared = lax.all_to_all(jnp.broadcast_to(packed[None], (count,) + packed.shape), "tm", 0, 0)
+    average = jnp.sum(shared[:, 0], axis=0) / total_frames
+    peak_value = jnp.max(shared[:, 1], axis=0)
+    drift = shared[:, 0] / local_frames - average
+    variance = jnp.sum(shared[:, 2] + local_frames * drift * drift, axis=0) / total_frames
     centred = series - average[:, None]
-    variance = lax.psum(jnp.sum(centred * centred, axis=1), "tm") / total_frames
     deviation = jnp.sqrt(variance + 1e-05)
     zscore = centred / deviation[:, None]
     live_count = jnp.maximum(jnp.sum(chan_mask).astype(jnp.float32), 1.0)

time: 159 us -> 81.6 us (0.51)
  blocking collectives: 94 us -> 0 us
  starting transfers between devices: 5.18 us -> 13.5 us
  waiting for transfers between devices: 22.7 us -> 29.1 us
    psum x2 -> x0, blocking collectives: 64.5 us -> none  [the longest x1 35 us: per_device(): totals = lax.psum(jnp.sum(series, axis=1), 'tm')]
    pmax x1 -> x0, blocking collectives: 29.5 us -> none  [per_device(): peak_value = lax.pmax(jnp.max(series, axis=1), 'tm')]
    all_to_all x0 -> x1, starting transfers between devices: none -> 8.3 us  [per_device(): lax.all_to_all(jnp.broadcast_to(packed[None], (count,) + packed.shape), '...]
    all_to_all x0 -> x1, waiting for transfers between devices: none -> 5.81 us  [per_device(): lax.all_to_all(jnp.broadcast_to(packed[None], (count,) + packed.shape), '...]
  transfers between devices with their start and end apart: 3 -> 4, of which waited for: 2 -> 3; matrix products, arithmetic and copies ran while one was open for 2% -> 3% of each run, Pallas kernels for 0% -> 0%
where the time goes in v1:
time: 81.6 us; the launch traced here: 81.3 us
  waiting for transfers between devices  29.1 us (36%)
  matrix products  17.3 us (21%)
  starting transfers between devices  13.5 us (17%)
  other arithmetic  8.93 us (11%)
  local copies, waits for them, and re-layouts  8.53 us (10%)
  between operations  2.31 us (3%)
  loops' own time  1.66 us (2%)
    ppermute x3, waiting for transfers between devices, passed_along(): lax.ppermute(value, axis, [(source, source + steps) for source in range(f...  23.3 us
    dot_general x13, matrix products, add_group(): jnp.einsum('dsk,skt->dt', selector, stacked, preferred_element_type=jnp.f...  11.5 us
    all_to_all x1, starting transfers between devices, per_device(): lax.all_to_all(jnp.broadcast_to(packed[None], (count,) + packed.shape), '...  8.3 us
    all_to_all x1, waiting for transfers between devices, per_device(): lax.all_to_all(jnp.broadcast_to(packed[None], (count,) + packed.shape), '...  5.81 us
    ppermute x3, starting transfers between devices, passed_along(): lax.ppermute(value, axis, [(source, source + steps) for source in range(f...  5.18 us
    while x91, local copies, waits for them, and re-layouts  3.45 us
    add x1, other arithmetic, per_device(): weighted + coeffs[tap_index] * extended[:, :, tap_index:tap_index + frame...  2.62 us
    unnamed x8, local copies, waits for them, and re-layouts  2.01 us
  transfers between devices with their start and end apart: 4, of which 3 were waited for; matrix products, arithmetic and copies ran while one was open for 3% of the time, Pallas kernels for 0%

profile of v1, /device:TPU:0, one launch (start us, length us, event | category | flops | bytes accessed | tf_op | source)
XLA Modules:
  0.0 81.3 jit_solution(9224142694779756181)
XLA Ops:
  0.6 1.4 %reshape.181 = bf16[2,2,32,2048]{3,2,1,0:T(8,128)(2,1)S(1)} reshape(bf16[2,2,65536]{2,1,0:T(2,128)(2,1)} %param.5) | data formatting | bytes 1048576 | tf_op jit(solution)/shard_map/reshape | solution.py:100
  2.2 2.4 %collective-permute-start = (bf16[2,2,15,2048]{3,2,0,1:T(8,128)(2,1)S(1)}, bf16[2,2,15,2048]{3,2,0,1:T(8,128)(2,1)S(1)}, u32[]{:S(2)}, u32[]{:S(2)}) collective-permute-start(bf16[2,2,15,2048]{3,2,0,1:T(8,128)(2,1)S(1)} %slice.230), channel_id=1, source_target_pairs={{0,1},{1,2},{2,3},{3,4},{4,5},{5,6},{6,7},{7,8},{8,9},{9,10},{10,1... | collective-permute-start | bytes 737288 | tf_op jit(solution)/shard_map/ppermute | solution.py:20
  4.6 1.2 %multiply_reduce_fusion = f32[]{:T(128)} fusion(), kind=kLoop, calls=%fused_computation.128 | loop fusion | flops 1343487 | bytes 4 | tf_op jit(solution)/shard_map/reduce_sum | solution.py:29
  8.0 2.6 %multiply_add_fusion = f32[2,2,32,2048]{3,2,0,1:T(8,128)S(1)} fusion(bf16[2,2,32,2048]{3,2,0,1:T(8,128)(2,1)S(1)} %copy.25, bf16[2,2,15,2048]{3,2,0,1:T(8,128)(2,1)S(1)} %collective-permute-done, f32[2048]{0:T(1024)S(1)} %get-tuple-element.141, f32[2048]{0:T(1024)S(1)} %get-tuple-element.142, f32[2048]{0:T(1024)S(1)} %get-tuple-element.143, ...), kind=kLoop, calls=%fused_computation.61 | loop fusion | flops 24117248 | bytes 1949696 | tf_op jit(solution)/shard_map/add | solution.py:106
  17.5 1.3 %collective-permute-start.1 = (bf16[2048,32]{1,0:T(8,128)(2,1)S(1)}, bf16[2048,32]{1,0:T(8,128)(2,1)S(1)}, u32[]{:S(2)}, u32[]{:S(2)}) collective-permute-start(bf16[2048,32]{1,0:T(8,128)(2,1)S(1)} %bitcast_multiply_fusion), channel_id=1, source_target_pairs={{1,0},{2,1},{3,2},{4,3},{5,4},{6,5},{7,6},{8,7},{9,8},{10,9},{11,1... | collective-permute-start | bytes 393224 | tf_op jit(solution)/shard_map/ppermute | solution.py:20
  18.8 4.6 %collective-permute-done.1 = bf16[2048,32]{1,0:T(8,128)(2,1)S(1)} collective-permute-done((bf16[2048,32]{1,0:T(8,128)(2,1)S(1)}, bf16[2048,32]{1,0:T(8,128)(2,1)S(1)}, u32[]{:S(2)}, u32[]{:S(2)}) %collective-permute-start.1) | collective-permute-done | bytes 131104 | tf_op jit(solution)/shard_map/ppermute | solution.py:20
  23.7 1.5 %collective-permute-start.2 = (bf16[2048,64]{1,0:T(8,128)(2,1)S(1)}, bf16[2048,64]{1,0:T(8,128)(2,1)S(1)}, u32[]{:S(2)}, u32[]{:S(2)}) collective-permute-start(bf16[2048,64]{1,0:T(8,128)(2,1)S(1)} %pad_maximum_fusion.1), channel_id=1, source_target_pairs={{2,0},{3,1},{4,2},{5,3},{6,4},{7,5},{8,6},{9,7},{10,8},{11,9},{12,... | collective-permute-start | bytes 786440 | tf_op jit(solution)/shard_map/ppermute | solution.py:20
  25.2 18.7 %collective-permute-done.2 = bf16[2048,64]{1,0:T(8,128)(2,1)S(1)} collective-permute-done((bf16[2048,64]{1,0:T(8,128)(2,1)S(1)}, bf16[2048,64]{1,0:T(8,128)(2,1)S(1)}, u32[]{:S(2)}, u32[]{:S(2)}) %collective-permute-start.2) | collective-permute-done | bytes 262176 | tf_op jit(solution)/shard_map/ppermute | solution.py:20
  43.9 0.9 %maximum_maximum_fusion = bf16[2048,136]{1,0:T(8,128)(2,1)S(1)} fusion(bf16[2048,64]{1,0:T(8,128)(2,1)S(1)} %collective-permute-done.2, bf16[2048,32]{1,0:T(8,128)(2,1)S(1)} %collective-permute-done.1, bf16[2048,32]{1,0:T(8,128)(2,1)S(1)} %bitcast_multiply_fusion, bf16[136]{0:T(256)(128)(2,1)S(1)} %pad.9.clone), kind=kLoop, calls=%fused_computation.60 | loop fusion | flops 2228224 | bytes 1081616 | tf_op jit(solution)/shard_map/concatenate | solution.py:77
  45.8 17.2 %while.14 = (s32[]{:T(128)}, f32[64,32]{0,1:T(8,128)S(1)}, s32[64,2048]{1,0:T(8,128)S(1)}, bf16[2048,136]{0,1:T(8,128)(2,1)S(1)}, s32[]{:T(128)}, /*index=5*/s32...) while((s32[]{:T(128)}, f32[64,32]{0,1:T(8,128)S(1)}, ...), condition=%wide.region_3.4_spmd.clone, body=%wide.region_2.3_spmd.clone.sunk | while | flops 68161560 | bytes 3686781 | solution.py:95
  46.2 0.9 %fusion.181 = f32[64,32]{0,1:T(8,128)S(1)} fusion(bf16[8,2048,32]{1,2,0:T(8,128)(2,1)S(1)} %fusion.180, s32[64,2048]{1,0:T(8,128)S(1)} %get-tuple-element.224, s32[8]{0:T(128)S(1)} %iota_add_fusion.3, f32[64,32]{0,1:T(8,128)S(1)} %get-tuple-element.208, pred[]{:T(512)S(6)} %compare.11), kind=kOutput, calls=%fused_computation.6.clone.1 | convolution fusion | flops 68161536 | bytes 1589281 | tf_op jit(solution)/shard_map/while/body/eval_jaxpr/dsk,skt->dt/dot_general | solution.py:90
  47.6 0.9 %fusion.181 = f32[64,32]{0,1:T(8,128)S(1)} fusion(bf16[8,2048,32]{1,2,0:T(8,128)(2,1)S(1)} %fusion.180, s32[64,2048]{1,0:T(8,128)S(1)} %get-tuple-element.224, s32[8]{0:T(128)S(1)} %iota_add_fusion.3, f32[64,32]{0,1:T(8,128)S(1)} %get-tuple-element.208, pred[]{:T(512)S(6)} %compare.11), kind=kOutput, calls=%fused_computation.6.clone.1 | convolution fusion | flops 68161536 | bytes 1589281 | tf_op jit(solution)/shard_map/while/body/eval_jaxpr/dsk,skt->dt/dot_general | solution.py:90
  48.9 0.9 %fusion.181 = f32[64,32]{0,1:T(8,128)S(1)} fusion(bf16[8,2048,32]{1,2,0:T(8,128)(2,1)S(1)} %fusion.180, s32[64,2048]{1,0:T(8,128)S(1)} %get-tuple-element.224, s32[8]{0:T(128)S(1)} %iota_add_fusion.3, f32[64,32]{0,1:T(8,128)S(1)} %get-tuple-element.208, pred[]{:T(512)S(6)} %compare.11), kind=kOutput, calls=%fused_computation.6.clone.1 | convolution fusion | flops 68161536 | bytes 1589281 | tf_op jit(solution)/shard_map/while/body/eval_jaxpr/dsk,skt->dt/dot_general | solution.py:90
  50.2 0.9 %fusion.181 = f32[64,32]{0,1:T(8,128)S(1)} fusion(bf16[8,2048,32]{1,2,0:T(8,128)(2,1)S(1)} %fusion.180, s32[64,2048]{1,0:T(8,128)S(1)} %get-tuple-element.224, s32[8]{0:T(128)S(1)} %iota_add_fusion.3, f32[64,32]{0,1:T(8,128)S(1)} %get-tuple-element.208, pred[]{:T(512)S(6)} %compare.11), kind=kOutput, calls=%fused_computation.6.clone.1 | convolution fusion | flops 68161536 | bytes 1589281 | tf_op jit(solution)/shard_map/while/body/eval_jaxpr/dsk,skt->dt/dot_general | solution.py:90
  51.6 0.9 %fusion.181 = f32[64,32]{0,1:T(8,128)S(1)} fusion(bf16[8,2048,32]{1,2,0:T(8,128)(2,1)S(1)} %fusion.180, s32[64,2048]{1,0:T(8,128)S(1)} %get-tuple-element.224, s32[8]{0:T(128)S(1)} %iota_add_fusion.3, f32[64,32]{0,1:T(8,128)S(1)} %get-tuple-element.208, pred[]{:T(512)S(6)} %compare.11), kind=kOutput, calls=%fused_computation.6.clone.1 | convolution fusion | flops 68161536 | bytes 1589281 | tf_op jit(solution)/shard_map/while/body/eval_jaxpr/dsk,skt->dt/dot_general | solution.py:90
  52.9 0.9 %fusion.181 = f32[64,32]{0,1:T(8,128)S(1)} fusion(bf16[8,2048,32]{1,2,0:T(8,128)(2,1)S(1)} %fusion.180, s32[64,2048]{1,0:T(8,128)S(1)} %get-tuple-element.224, s32[8]{0:T(128)S(1)} %iota_add_fusion.3, f32[64,32]{0,1:T(8,128)S(1)} %get-tuple-element.208, pred[]{:T(512)S(6)} %compare.11), kind=kOutput, calls=%fused_computation.6.clone.1 | convolution fusion | flops 68161536 | bytes 1589281 | tf_op jit(solution)/shard_map/while/body/eval_jaxpr/dsk,skt->dt/dot_general | solution.py:90
  54.2 0.9 %fusion.181 = f32[64,32]{0,1:T(8,128)S(1)} fusion(bf16[8,2048,32]{1,2,0:T(8,128)(2,1)S(1)} %fusion.180, s32[64,2048]{1,0:T(8,128)S(1)} %get-tuple-element.224, s32[8]{0:T(128)S(1)} %iota_add_fusion.3, f32[64,32]{0,1:T(8,128)S(1)} %get-tuple-element.208, pred[]{:T(512)S(6)} %compare.11), kind=kOutput, calls=%fused_computation.6.clone.1 | convolution fusion | flops 68161536 | bytes 1589281 | tf_op jit(solution)/shard_map/while/body/eval_jaxpr/dsk,skt->dt/dot_general | solution.py:90
  55.5 0.9 %fusion.181 = f32[64,32]{0,1:T(8,128)S(1)} fusion(bf16[8,2048,32]{1,2,0:T(8,128)(2,1)S(1)} %fusion.180, s32[64,2048]{1,0:T(8,128)S(1)} %get-tuple-element.224, s32[8]{0:T(128)S(1)} %iota_add_fusion.3, f32[64,32]{0,1:T(8,128)S(1)} %get-tuple-element.208, pred[]{:T(512)S(6)} %compare.11), kind=kOutput, calls=%fused_computation.6.clone.1 | convolution fusion | flops 68161536 | bytes 1589281 | tf_op jit(solution)/shard_map/while/body/eval_jaxpr/dsk,skt->dt/dot_general | solution.py:90
  56.9 0.9 %fusion.181 = f32[64,32]{0,1:T(8,128)S(1)} fusion(bf16[8,2048,32]{1,2,0:T(8,128)(2,1)S(1)} %fusion.180, s32[64,2048]{1,0:T(8,128)S(1)} %get-tuple-element.224, s32[8]{0:T(128)S(1)} %iota_add_fusion.3, f32[64,32]{0,1:T(8,128)S(1)} %get-tuple-element.208, pred[]{:T(512)S(6)} %compare.11), kind=kOutput, calls=%fused_computation.6.clone.1 | convolution fusion | flops 68161536 | bytes 1589281 | tf_op jit(solution)/shard_map/while/body/eval_jaxpr/dsk,skt->dt/dot_general | solution.py:90
  58.2 0.9 %fusion.181 = f32[64,32]{0,1:T(8,128)S(1)} fusion(bf16[8,2048,32]{1,2,0:T(8,128)(2,1)S(1)} %fusion.180, s32[64,2048]{1,0:T(8,128)S(1)} %get-tuple-element.224, s32[8]{0:T(128)S(1)} %iota_add_fusion.3, f32[64,32]{0,1:T(8,128)S(1)} %get-tuple-element.208, pred[]{:T(512)S(6)} %compare.11), kind=kOutput, calls=%fused_computation.6.clone.1 | convolution fusion | flops 68161536 | bytes 1589281 | tf_op jit(solution)/shard_map/while/body/eval_jaxpr/dsk,skt->dt/dot_general | solution.py:90
  60.9 0.9 %fusion.181 = f32[64,32]{0,1:T(8,128)S(1)} fusion(bf16[8,2048,32]{1,2,0:T(8,128)(2,1)S(1)} %fusion.180, s32[64,2048]{1,0:T(8,128)S(1)} %get-tuple-element.224, s32[8]{0:T(128)S(1)} %iota_add_fusion.3, f32[64,32]{0,1:T(8,128)S(1)} %get-tuple-element.208, pred[]{:T(512)S(6)} %compare.11), kind=kOutput, calls=%fused_computation.6.clone.1 | convolution fusion | flops 68161536 | bytes 1589281 | tf_op jit(solution)/shard_map/while/body/eval_jaxpr/dsk,skt->dt/dot_general | solution.py:90
  62.2 0.9 %fusion.181 = f32[64,32]{0,1:T(8,128)S(1)} fusion(bf16[8,2048,32]{1,2,0:T(8,128)(2,1)S(1)} %fusion.180, s32[64,2048]{1,0:T(8,128)S(1)} %get-tuple-element.224, s32[8]{0:T(128)S(1)} %iota_add_fusion.3, f32[64,32]{0,1:T(8,128)S(1)} %get-tuple-element.208, pred[]{:T(512)S(6)} %compare.11), kind=kOutput, calls=%fused_computation.6.clone.1 | convolution fusion | flops 68161536 | bytes 1589281 | tf_op jit(solution)/shard_map/while/body/eval_jaxpr/dsk,skt->dt/dot_general | solution.py:90
  63.9 8.3 %all-to-all-start = ((f32[16,1,192]{2,1,0:T(1,128)}), f32[16,1,192]{2,1,0:T(1,128)S(1)}, u32[]{:S(2)}, u32[]{:S(2)}) async-start(f32[16,1,192]{2,1,0:T(1,128)} %reshape.188), calls=%async_computation | async-start | bytes 32768 | tf_op jit(solution)/shard_map/all_to_all | solution.py:127
  72.9 5.8 %all-to-all-done = f32[16,1,192]{2,1,0:T(1,128)S(1)} async-done(((f32[16,1,192]{2,1,0:T(1,128)}), f32[16,1,192]{2,1,0:T(1,128)S(1)}, u32[]{:S(2)}, u32[]{:S(2)}) %all-to-all-start) | async-done | bytes 12320 | tf_op jit(solution)/shard_map/all_to_all | solution.py:127
  (162 shorter events, 17.9 us)
Async XLA Ops:
  2.0 5.2 %copy-start = (s32[2048]{0:T(1024)S(1)}, s32[2048]{0:T(1024)}, u32[]{:S(2)}) copy-start(s32[2048]{0:T(1024)} %param.7) | copy-start | bytes 24580
  2.2 5.8 %collective-permute-start = (bf16[2,2,15,2048]{3,2,0,1:T(8,128)(2,1)S(1)}, bf16[2,2,15,2048]{3,2,0,1:T(8,128)(2,1)S(1)}, u32[]{:S(2)}, u32[]{:S(2)}) collective-permute-start(bf16[2,2,15,2048]{3,2,0,1:T(8,128)(2,1)S(1)} %slice.230), channel_id=1, source_target_pairs={{0,1},{1,2},{2,3},{3,4},{4,5},{5,6},{6,7},{7,8},{8,9},{9,10},{10,1... | collective-permute-start | bytes 737288 | tf_op jit(solution)/shard_map/ppermute | solution.py:20
  17.5 5.9 %collective-permute-start.1 = (bf16[2048,32]{1,0:T(8,128)(2,1)S(1)}, bf16[2048,32]{1,0:T(8,128)(2,1)S(1)}, u32[]{:S(2)}, u32[]{:S(2)}) collective-permute-start(bf16[2048,32]{1,0:T(8,128)(2,1)S(1)} %bitcast_multiply_fusion), channel_id=1, source_target_pairs={{1,0},{2,1},{3,2},{4,3},{5,4},{6,5},{7,6},{8,7},{9,8},{10,9},{11,1... | collective-permute-start | bytes 393224 | tf_op jit(solution)/shard_map/ppermute | solution.py:20
  23.7 20.2 %collective-permute-start.2 = (bf16[2048,64]{1,0:T(8,128)(2,1)S(1)}, bf16[2048,64]{1,0:T(8,128)(2,1)S(1)}, u32[]{:S(2)}, u32[]{:S(2)}) collective-permute-start(bf16[2048,64]{1,0:T(8,128)(2,1)S(1)} %pad_maximum_fusion.1), channel_id=1, source_target_pairs={{2,0},{3,1},{4,2},{5,3},{6,4},{7,5},{8,6},{9,7},{10,8},{11,9},{12,... | collective-permute-start | bytes 786440 | tf_op jit(solution)/shard_map/ppermute | solution.py:20
  44.8 1.0 %copy-start.1 = (s32[64,2048]{1,0:T(8,128)S(1)}, s32[64,2048]{1,0:T(8,128)}, u32[]{:S(2)}) copy-start(s32[64,2048]{1,0:T(8,128)} %param.6) | copy-start | bytes 1572868
  63.9 14.8 %all-to-all-start = ((f32[16,1,192]{2,1,0:T(1,128)}), f32[16,1,192]{2,1,0:T(1,128)S(1)}, u32[]{:S(2)}, u32[]{:S(2)}) async-start(f32[16,1,192]{2,1,0:T(1,128)} %reshape.188), calls=%async_computation | async-start | bytes 32768 | tf_op jit(solution)/shard_map/all_to_all | solution.py:127

commit v2 on v0

v2 whole, which is shorter than its diff:
```python
import math

import jax
import jax.numpy as jnp
import numpy as np
from jax import lax
from jax.experimental import pallas as pl
from jax.experimental.pallas import tpu as pltpu
from jax.sharding import PartitionSpec as P

NCHAN = 2048
TAPS = 16
DSPAN = 3
LANES = 128
RADIX = NCHAN // LANES
GROUP = 8
TILE = 256
NTILE = NCHAN // TILE
CHUNK = 4

f32 = jnp.float32
bf16 = jnp.bfloat16


def split_pair(table):
    table = np.asarray(table, np.float32)
    high = table.astype(jnp.bfloat16)
    low = (table - high.astype(np.float32)).astype(jnp.bfloat16)
    return np.stack([high, low])


def make_tables():
    length = TAPS * NCHAN
    position = np.arange(length, dtype=np.float64)
    window = 0.54 - 0.46 * np.cos(2.0 * np.pi * position / (length - 1))
    shaped = np.sinc((position - (length - 1) / 2.0) / NCHAN) * window
    shaped = shaped * np.sqrt(NCHAN / np.sum(shaped * shaped))
    coeffs = shaped.reshape(TAPS * RADIX, LANES).astype(np.float32)
    rows = np.arange(RADIX)
    angle = 2.0 * np.pi * np.outer(rows, rows) / RADIX
    eye = np.eye(GROUP)
    cos_one, sin_one = np.kron(eye, np.cos(angle)), np.kron(eye, np.sin(angle))
    first = split_pair(np.block([[cos_one, sin_one], [-sin_one, cos_one]]))
    lanes = np.arange(LANES)
    angle = 2.0 * np.pi * np.outer(rows, lanes) / NCHAN
    twist = np.stack([np.tile(np.cos(angle), (GROUP, 1)), np.tile(np.sin(angle), (GROUP, 1))])
    angle = 2.0 * np.pi * np.outer(lanes, lanes) / LANES
    scale = 1.0 / math.sqrt(NCHAN)
    cos_two, sin_two = scale * np.cos(angle), scale * np.sin(angle)
    second = split_pair(np.block([[cos_two, -sin_two], [sin_two, cos_two]]))
    low_count = TILE // RADIX
    order = np.zeros((TILE, TILE), np.float32)
    for k_one in range(RADIX):
        for k_low in range(low_count):
            order[k_low * RADIX + k_one, k_one * low_count + k_low] = 1.0
    return coeffs, first, twist.astype(np.float32), second, order.astype(jnp.bfloat16)


def halves(value):
    high = value.astype(bf16)
    return high, (value - high.astype(f32)).astype(bf16)


def dot(left, right):
    return jnp.dot(left, right, preferred_element_type=f32)


def roll_left(value, steps):
    width = value.shape[-1]
    return pltpu.roll(value, (width - steps) % width, axis=value.ndim - 1)


def prep_kernel(delays_ref, mask_ref, order_ref, rel_ref, base_ref, reach_ref):
    order = order_ref[...]
    for tile in range(NTILE):
        here = delays_ref[:, tile * TILE : (tile + 1) * TILE]
        least = here[:, TILE - 1 : TILE]
        live = mask_ref[:, tile * TILE : (tile + 1) * TILE] > 0
        rel = jnp.where(live, here - least, -1).astype(f32).astype(bf16)
        rel_ref[:, tile * TILE : (tile + 1) * TILE] = dot(rel, order)
        base_ref[tile] = jnp.broadcast_to(least, base_ref.shape[1:])
        reach_ref[tile] = jnp.max(here[:, 0:1] - least)


def main_kernel(reach_ref, x_ref, hist_ref, coeffs_ref, first_ref, twist_ref, second_ref, rel_ref,
                base_ref, out_ref, ext_ref, weighted_ref, det_ref, tile_ref, acc_ref):
    frames = x_ref.shape[1] // RADIX
    past = (TAPS - 1) * RADIX
    for plane in range(4):
        ext_ref[plane, :past] = hist_ref[plane].astype(f32)
        ext_ref[plane, past:] = x_ref[plane].astype(f32)
    tile_ref[...] = jnp.zeros_like(tile_ref)

    for half in range(RADIX // 8):
        taps = [coeffs_ref[tap * RADIX + half * 8 : tap * RADIX + half * 8 + 8] for tap in range(TAPS)]

        def weigh(group, carry):
            for plane in range(4):
                pol, part = divmod(plane, 2)
                for inner in range(GROUP):
                    start = pl.multiple_of((group * GROUP + inner) * RADIX + half * 8, 8)
                    total = None
                    for tap in range(TAPS):
                        term = taps[tap] * ext_ref[plane, pl.ds(start + tap * RADIX, 8)]
                        total = term if total is None else total + term
                    row = part * GROUP * RADIX + inner * RADIX + half * 8
                    weighted_ref[group, row : row + 8, pol * LANES : (pol + 1) * LANES] = total
            return carry

        lax.fori_loop(0, frames // GROUP, weigh, 0)

    span = GROUP * RADIX
    twist_cos, twist_sin = twist_ref[0], twist_ref[1]
    for group in range(frames // GROUP):
        high, low = halves(weighted_ref[group])
        mixed = dot(first_ref[0], high) + dot(first_ref[0], low) + dot(first_ref[1], high)
        energy = None
        for pol in range(2):
            real = mixed[:span, pol * LANES : (pol + 1) * LANES]
            imag = mixed[span:, pol * LANES : (pol + 1) * LANES]
            turned = jnp.concatenate(
                [real * twist_cos + imag * twist_sin, imag * twist_cos - real * twist_sin], axis=1
            )
            high, low = halves(turned)
            final = dot(high, second_ref[0]) + dot(low, second_ref[0]) + dot(high, second_ref[1])
            square = final * final
            power = square[:, :LANES] + square[:, LANES:]
            energy = power if energy is None else energy + power
        det_ref[group * span : (group + 1) * span] = energy.astype(bf16).astype(f32)

    width = LANES // 8
    lane_group = lax.broadcasted_iota(jnp.int32, (frames, LANES), 1) // width
    for half in range(RADIX // 8):
        rows = [det_ref[pl.ds(half * 8 + index, frames, stride=RADIX), :] for index in range(8)]
        for bit in (4, 2, 1):
            upper = (lane_group & bit) != 0
            for index in range(8):
                if index & bit:
                    continue
                one, two = rows[index], rows[index + bit]
                rows[index] = jnp.where(upper, pltpu.roll(two, bit * width, axis=1), one)
                rows[index + bit] = jnp.where(upper, two, roll_left(one, bit * width))
        for tile in range(NTILE):
            tile_ref[tile, DSPAN * frames :, half * LANES : (half + 1) * LANES] = rows[tile].astype(bf16)

    trials = rel_ref.shape[0]
    acc_ref[...] = jnp.zeros_like(acc_ref)
    most = reach_ref[0]
    for tile in range(1, NTILE):
        most = jnp.maximum(most, reach_ref[tile])
    steps = most // CHUNK + 1

    def add_chunk(step, carry):
        lowest = (steps - 1 - step) * CHUNK
        for tile in range(NTILE):
            rel = rel_ref[:, tile * TILE : (tile + 1) * TILE]
            chosen = jnp.concatenate(
                [
                    jnp.where(rel == (lowest + offset).astype(f32), 1.0, 0.0).astype(bf16)
                    for offset in range(CHUNK)
                ],
                axis=0,
            )
            sums = lax.dot_general(
                chosen, tile_ref[tile], (((1,), (1,)), ((), ())), preferred_element_type=f32
            )
            acc = acc_ref[tile]
            for offset in reversed(range(CHUNK)):
                acc = roll_left(acc, 1) + sums[offset * trials : (offset + 1) * trials]
            acc_ref[tile] = acc
        return carry

    lax.fori_loop(0, steps, add_chunk, 0)

    total = None
    for tile in range(NTILE):
        base = base_ref[tile]
        value = acc_ref[tile]
        bit = 1
        while bit <= DSPAN * frames:
            value = jnp.where((base & bit) != 0, roll_left(value, bit), value)
            bit *= 2
        total = value if total is None else total + value
    out_ref[...] = total


def stats_kernel(where_ref, parts_ref, mask_ref, zscore_ref, stats_ref):
    count, trials, width = parts_ref.shape
    frames = zscore_ref.shape[1]
    share = width // frames
    lane = lax.broadcasted_iota(jnp.int32, (trials, width), 1)
    block = lane // frames
    sums = [None] * (count // share)

    def put(index, value):
        sums[index] = value if sums[index] is None else sums[index] + value

    for device in range(count):
        part = parts_ref[device]
        turn = frames * ((device + 1) % share)
        if turn:
            part = pltpu.roll(part, turn, axis=1)
        group, within = divmod(device, share)
        stays = block <= within
        put(group, jnp.where(stays, part, 0.0))
        if group > 0 and within < share - 1:
            put(group - 1, jnp.where(stays, 0.0, part))
    total_frames = float(count * frames)
    whole, peak = sums[0], sums[0]
    for part in sums[1:]:
        whole = whole + part
        peak = jnp.maximum(peak, part)
    average = jnp.sum(whole, axis=1, keepdims=True) / total_frames
    peak_value = jnp.max(peak, axis=1, keepdims=True)
    squares = None
    mine = jnp.zeros((trials, width), f32)
    own_group = where_ref[0] // share
    for index, part in enumerate(sums):
        centred = part - average
        square = centred * centred
        squares = square if squares is None else squares + square
        mine = jnp.where(own_group == index, centred, mine)
    variance = jnp.sum(squares, axis=1, keepdims=True) / total_frames
    deviation = jnp.sqrt(variance + 1e-05)
    own_block = where_ref[0] % share
    picked = None
    for index in range(share):
        piece = jnp.where(own_block == index, mine[:, index * frames : (index + 1) * frames], 0.0)
        picked = piece if picked is None else picked + piece
    zscore_ref[...] = picked / deviation
    live = jnp.sum(mask_ref[...].astype(f32), axis=1, keepdims=True)
    live = jnp.maximum(live, 1.0)
    row = lax.broadcasted_iota(jnp.int32, (trials, width), 0)
    for index, column in enumerate((average / live, deviation / live, (peak_value - average) / deviation)):
        spread = jnp.where(row == lane, column, 0.0)
        stats_ref[index : index + 1, :] = jnp.sum(spread, axis=0, keepdims=True)[:, :trials]


def per_device(voltage, delays, chan_mask):
    frames = voltage.shape[2] // NCHAN
    trials = delays.shape[0]
    coeffs, first, twist, second, order = make_tables()
    framed = voltage.reshape(4, frames * RADIX, LANES)
    count = lax.axis_size("tm")
    hist = lax.ppermute(
        framed[:, (frames - TAPS + 1) * RADIX :], "tm", [(i, i + 1) for i in range(count - 1)]
    )
    mask_row = chan_mask.reshape(1, NCHAN)
    vmem = pl.BlockSpec(memory_space=pltpu.VMEM)
    smem = pl.BlockSpec(memory_space=pltpu.SMEM)
    rel, base, reach = pl.pallas_call(
        prep_kernel,
        name="prep",
        out_shape=(
            jax.ShapeDtypeStruct((trials, NCHAN), f32),
            jax.ShapeDtypeStruct((NTILE, trials, LANES), jnp.int32),
            jax.ShapeDtypeStruct((NTILE,), jnp.int32),
        ),
        in_specs=[vmem] * 3,
        out_specs=(vmem, vmem, smem),
    )(delays, mask_row, order)
    window = (DSPAN + 1) * frames
    partial = pl.pallas_call(
        main_kernel,
        name="channelize",
        out_shape=jax.ShapeDtypeStruct((trials, window), f32),
        in_specs=[smem] + [vmem] * 8,
        out_specs=vmem,
        scratch_shapes=[
            pltpu.VMEM((4, (frames + TAPS - 1) * RADIX, LANES), f32),
            pltpu.VMEM((frames // GROUP, 2 * GROUP * RADIX, 2 * LANES), f32),
            pltpu.VMEM((frames * RADIX, LANES), f32),
            pltpu.VMEM((NTILE, window, TILE), bf16),
            pltpu.VMEM((NTILE, trials, window), f32),
        ],
    )(reach, framed, hist, coeffs, first, twist, second, rel, base)
    parts = lax.all_to_all(jnp.broadcast_to(partial[None], (count, trials, window)), "tm", 0, 0)
    here = lax.axis_index("tm").astype(jnp.int32).reshape(1)
    return pl.pallas_call(
        stats_kernel,
        name="normalize",
        out_shape=(
            jax.ShapeDtypeStruct((trials, frames), f32),
            jax.ShapeDtypeStruct((3, trials), f32),
        ),
        in_specs=[smem, vmem, vmem],
        out_specs=(vmem, vmem),
    )(here, parts, mask_row)


def solution(mesh):
    in_specs = (P(None, None, ("beam", "tm")), P(), P("beam"))
    out_specs = (P(None, ("beam", "tm")), P(None, "beam"))
    return jax.shard_map(
        per_device, mesh=mesh, in_specs=in_specs, out_specs=out_specs, check_vma=False
    )
```

time: 159 us -> 47.5 us (0.30)
  blocking collectives: 94 us -> 0 us
  matrix products: 17.3 us -> 0 us
  Pallas kernels: 0 us -> 13.6 us
  waiting for transfers between devices: 22.7 us -> 14.3 us
  other arithmetic: 8.09 us -> 0 us
  starting transfers between devices: 5.18 us -> 12.5 us
  loops' own time: 1.66 us -> 0 us
    psum x2 -> x0, blocking collectives: 64.5 us -> none  [the longest x1 35 us: per_device(): totals = lax.psum(jnp.sum(series, axis=1), 'tm')]
    pmax x1 -> x0, blocking collectives: 29.5 us -> none  [per_device(): peak_value = lax.pmax(jnp.max(series, axis=1), 'tm')]
    ppermute x3 -> x1, waiting for transfers between devices: 22.7 us -> 0.01 us  [per_device(): lax.ppermute(framed[:, (frames - TAPS + 1) * RADIX:], 'tm', [(i, i + 1) f...]
    dot_general x21 -> x0, matrix products: 17.3 us -> none  [the longest x13 11.5 us: add_group(): jnp.einsum('dsk,skt->dt', selector, stacked, preferred_element_type=jnp.f...]
    all_to_all x0 -> x1, waiting for transfers between devices: none -> 14.3 us  [per_device(): lax.all_to_all(jnp.broadcast_to(partial[None], (count, trials, window)),...]
    pallas_call x0 -> x3, Pallas kernels: none -> 13.6 us  [the longest x1 9.18 us: per_device(): pl.pallas_call(main_kernel, name='channelize', out_shape=jax.ShapeDtypeSt...]
    all_to_all x0 -> x1, starting transfers between devices: none -> 10.1 us  [per_device(): lax.all_to_all(jnp.broadcast_to(partial[None], (count, trials, window)),...]
    while x91 -> x0, local copies, waits for them, and re-layouts: 3.45 us -> none
  transfers between devices with their start and end apart: 3 -> 2, of which waited for: 2 -> 1; matrix products, arithmetic and copies ran while one was open for 2% -> 0% of each run, Pallas kernels for 0% -> 5%
where the time goes in v2:
time: 47.5 us; the launch traced here: 47 us
  waiting for transfers between devices  14.3 us (30%)
  Pallas kernels  13.6 us (29%)
  starting transfers between devices  12.5 us (26%)
  local copies, waits for them, and re-layouts  5.91 us (12%)
  between operations  0.71 us (1%)
    all_to_all x1, waiting for transfers between devices, per_device(): lax.all_to_all(jnp.broadcast_to(partial[None], (count, trials, window)),...  14.3 us
    all_to_all x1, starting transfers between devices, per_device(): lax.all_to_all(jnp.broadcast_to(partial[None], (count, trials, window)),...  10.1 us
    pallas_call x1, Pallas kernels, per_device(): pl.pallas_call(main_kernel, name='channelize', out_shape=jax.ShapeDtypeSt...  9.18 us
    pallas_call x1, Pallas kernels, per_device(): pl.pallas_call(prep_kernel, name='prep', out_shape=(jax.ShapeDtypeStruct(...  2.42 us
    ppermute x1, starting transfers between devices, per_device(): lax.ppermute(framed[:, (frames - TAPS + 1) * RADIX:], 'tm', [(i, i + 1) f...  2.41 us
    pallas_call x1, Pallas kernels, per_device(): pl.pallas_call(stats_kernel, name='normalize', out_shape=(jax.ShapeDtypeS...  2.02 us
    broadcast_in_dim x1, local copies, waits for them, and re-layouts, per_device(): jnp.broadcast_to(partial[None], (count, trials, window))  1.6 us
    unnamed x6, local copies, waits for them, and re-layouts  1.47 us
  transfers between devices with their start and end apart: 2, of which 1 were waited for; matrix products, arithmetic and copies ran while one was open for 0% of the time, Pallas kernels for 5%

profile of v2, /device:TPU:0, one launch (start us, length us, event | category | flops | bytes accessed | tf_op | source)
XLA Modules:
  0.0 47.0 jit_solution(12741142184024447328)
XLA Ops:
  0.6 1.4 %reshape.16.x_ref = bf16[4,512,128]{2,1,0:T(8,128)(2,1)S(1)} reshape(bf16[2,2,65536]{2,1,0:T(2,128)(2,1)} %param.8) | data formatting | bytes 1048576 | tf_op jit(solution)/shard_map/reshape | solution.py:243
  2.0 0.0 copy-start
  2.1 2.4 %collective-permute-start = (bf16[4,240,128]{2,1,0:T(8,128)(2,1)S(1)}, bf16[4,240,128]{2,1,0:T(8,128)(2,1)S(1)}, u32[]{:S(2)}, u32[]{:S(2)}) collective-permute-start(bf16[4,240,128]{2,1,0:T(8,128)(2,1)S(1)} %slice.4), channel_id=1, source_target_pairs={{0,1},{1,2},{2,3},{3,4},{4,5},{5,6},{6,7},{7,8},{8,9},{9,10},{10,1... | collective-permute-start | bytes 737288 | tf_op jit(solution)/shard_map/ppermute | solution.py:245
  4.5 2.4 %prep.1 = (f32[64,2048]{1,0:T(8,128)}, s32[8,64,128]{2,1,0:T(8,128)}, s32[8]{0:T(128)}) custom-call(s32[64,2048]{1,0:T(8,128)} %delays_ref.1, s32[1,2048]{1,0:T(1,128)} %bitcast.2, bf16[256,256]{1,0:T(8,128)(2,1)} %constant.14.clone.order_ref), custom_call_target="tpu_custom_call" | custom-call | tf_op jit(solution)/shard_map/prep/pallas_call | solution.py:251
  6.9 0.0 copy-done
  6.9 0.0 collective-permute-done.hist_ref
  6.9 0.0 copy-start.2
  6.9 0.7 %copy-done.2 = bf16[4,240,128]{2,1,0:T(8,128)(2,1)} copy-done((bf16[4,240,128]{2,1,0:T(8,128)(2,1)}, bf16[4,240,128]{2,1,0:T(8,128)(2,1)S(1)}, u32[]{:S(2)}) %copy-start.2) | copy-done | bytes 245784
  7.6 9.2 %channelize.1 = f32[64,128]{1,0:T(8,128)} custom-call(s32[8]{0:T(128)} %get-tuple-element.5.reach_ref, bf16[4,512,128]{2,1,0:T(8,128)(2,1)} %copy-done, bf16[4,240,128]{2,1,0:T(8,128)(2,1)} %copy-done.2, f32[256,128]{1,0:T(8,128)} %constant.15.clone.coeffs_ref, bf16[2,256,256]{2,1,0:T(8,128)(2,1)} %constant.16.clone.first_ref, ...), custom_call_target="tpu_custom_call" | custom-call | tf_op jit(solution)/shard_map/channelize/pallas_call | solution.py:263
  16.8 1.6 %broadcast_in_dim.2 = f32[16,64,128]{2,1,0:T(8,128)} broadcast(f32[64,128]{1,0:T(8,128)} %channelize.1), dimensions={1,2} | broadcast | bytes 557056 | tf_op jit(solution)/shard_map/broadcast_in_dim | solution.py:277
  18.4 10.1 %all-to-all-start = ((f32[16,64,128]{2,1,0:T(8,128)}), f32[16,64,128]{2,1,0:T(8,128)S(1)}, u32[]{:S(2)}, u32[]{:S(2)}) async-start(f32[16,64,128]{2,1,0:T(8,128)} %broadcast_in_dim.2), calls=%async_computation | async-start | bytes 1048576 | tf_op jit(solution)/shard_map/all_to_all | solution.py:277
  28.5 14.3 %all-to-all-done.parts_ref = f32[16,64,128]{2,1,0:T(8,128)S(1)} async-done(((f32[16,64,128]{2,1,0:T(8,128)}), f32[16,64,128]{2,1,0:T(8,128)S(1)}, u32[]{:S(2)}, u32[]{:S(2)}) %all-to-all-start) | async-done | bytes 524320 | tf_op jit(solution)/shard_map/all_to_all | solution.py:277
  42.8 0.0 copy-start.1
  42.8 0.8 %copy-done.1 = f32[16,64,128]{2,1,0:T(8,128)} copy-done((f32[16,64,128]{2,1,0:T(8,128)}, f32[16,64,128]{2,1,0:T(8,128)S(1)}, u32[]{:S(2)}) %copy-start.1) | copy-done | bytes 524312
  43.6 2.0 %normalize.1 = (f32[64,32]{1,0:T(8,128)}, f32[3,64]{1,0:T(4,128)}) custom-call(s32[1]{0:T(128)} %bitcast.where_ref, f32[16,64,128]{2,1,0:T(8,128)} %copy-done.1, s32[1,2048]{1,0:T(1,128)} %bitcast.3), custom_call_target="tpu_custom_call" | custom-call | tf_op jit(solution)/shard_map/normalize/pallas_call | solution.py:279
  45.6 1.4 %copy.10 = f32[64,32]{0,1:T(8,128)} copy(f32[64,32]{1,0:T(8,128)} %get-tuple-element.8) | data formatting | bytes 16384 | tf_op jit(solution)/shard_map/normalize/pallas_call | solution.py:279
  (1 shorter events, 0.0 us)
Async XLA Ops:
  2.0 4.9 %copy-start = (bf16[4,512,128]{2,1,0:T(8,128)(2,1)}, bf16[4,512,128]{2,1,0:T(8,128)(2,1)S(1)}, u32[]{:S(2)}) copy-start(bf16[4,512,128]{2,1,0:T(8,128)(2,1)S(1)} %reshape.16.x_ref) | copy-start | bytes 1572868
  2.1 4.9 %collective-permute-start = (bf16[4,240,128]{2,1,0:T(8,128)(2,1)S(1)}, bf16[4,240,128]{2,1,0:T(8,128)(2,1)S(1)}, u32[]{:S(2)}, u32[]{:S(2)}) collective-permute-start(bf16[4,240,128]{2,1,0:T(8,128)(2,1)S(1)} %slice.4), channel_id=1, source_target_pairs={{0,1},{1,2},{2,3},{3,4},{4,5},{5,6},{6,7},{7,8},{8,9},{9,10},{10,1... | collective-permute-start | bytes 737288 | tf_op jit(solution)/shard_map/ppermute | solution.py:245
  6.9 0.7 %copy-start.2 = (bf16[4,240,128]{2,1,0:T(8,128)(2,1)}, bf16[4,240,128]{2,1,0:T(8,128)(2,1)S(1)}, u32[]{:S(2)}) copy-start(bf16[4,240,128]{2,1,0:T(8,128)(2,1)S(1)} %collective-permute-done.hist_ref) | copy-start | bytes 737284
  18.4 24.4 %all-to-all-start = ((f32[16,64,128]{2,1,0:T(8,128)}), f32[16,64,128]{2,1,0:T(8,128)S(1)}, u32[]{:S(2)}, u32[]{:S(2)}) async-start(f32[16,64,128]{2,1,0:T(8,128)} %broadcast_in_dim.2), calls=%async_computation | async-start | bytes 1048576 | tf_op jit(solution)/shard_map/all_to_all | solution.py:277
  42.8 0.8 %copy-start.1 = (f32[16,64,128]{2,1,0:T(8,128)}, f32[16,64,128]{2,1,0:T(8,128)S(1)}, u32[]{:S(2)}) copy-start(f32[16,64,128]{2,1,0:T(8,128)S(1)} %all-to-all-done.parts_ref) | copy-start | bytes 1572868

commit v3 on v2

--- a/solution.py
+++ b/solution.py
@@ -16,7 +16,8 @@
 GROUP = 8
 TILE = 256
 NTILE = NCHAN // TILE
-CHUNK = 4
+CHUNK = 6
+GRANT = 16 * 1024 * 1024
 
 f32 = jnp.float32
 bf16 = jnp.bfloat16
@@ -77,7 +78,7 @@
         least = here[:, TILE - 1 : TILE]
         live = mask_ref[:, tile * TILE : (tile + 1) * TILE] > 0
         rel = jnp.where(live, here - least, -1).astype(f32).astype(bf16)
-        rel_ref[:, tile * TILE : (tile + 1) * TILE] = dot(rel, order)
+        rel_ref[:, tile * TILE : (tile + 1) * TILE] = dot(rel, order).astype(bf16)
         base_ref[tile] = jnp.broadcast_to(least, base_ref.shape[1:])
         reach_ref[tile] = jnp.max(here[:, 0:1] - least)
 
@@ -149,6 +150,8 @@
     for tile in range(1, NTILE):
         most = jnp.maximum(most, reach_ref[tile])
     steps = most // CHUNK + 1
+    one = jnp.ones((trials, TILE), bf16)
+    zero = jnp.zeros((trials, TILE), bf16)
 
     def add_chunk(step, carry):
         lowest = (steps - 1 - step) * CHUNK
@@ -156,7 +159,7 @@
             rel = rel_ref[:, tile * TILE : (tile + 1) * TILE]
             chosen = jnp.concatenate(
                 [
-                    jnp.where(rel == (lowest + offset).astype(f32), 1.0, 0.0).astype(bf16)
+                    jnp.where(rel == (lowest + offset).astype(f32).astype(bf16), one, zero)
                     for offset in range(CHUNK)
                 ],
                 axis=0,
@@ -181,12 +184,13 @@
             value = jnp.where((base & bit) != 0, roll_left(value, bit), value)
             bit *= 2
         total = value if total is None else total + value
-    out_ref[...] = total
+    for device in range(out_ref.shape[0]):
+        out_ref[device] = total
 
 
 def stats_kernel(where_ref, parts_ref, mask_ref, zscore_ref, stats_ref):
     count, trials, width = parts_ref.shape
-    frames = zscore_ref.shape[1]
+    frames = zscore_ref.shape[0]
     share = width // frames
     lane = lax.broadcasted_iota(jnp.int32, (trials, width), 1)
     block = lane // frames
@@ -223,11 +227,12 @@
     variance = jnp.sum(squares, axis=1, keepdims=True) / total_frames
     deviation = jnp.sqrt(variance + 1e-05)
     own_block = where_ref[0] % share
+    scaled = (mine / deviation).T
     picked = None
     for index in range(share):
-        piece = jnp.where(own_block == index, mine[:, index * frames : (index + 1) * frames], 0.0)
+        piece = jnp.where(own_block == index, scaled[index * frames : (index + 1) * frames], 0.0)
         picked = piece if picked is None else picked + piece
-    zscore_ref[...] = picked / deviation
+    zscore_ref[...] = picked
     live = jnp.sum(mask_ref[...].astype(f32), axis=1, keepdims=True)
     live = jnp.maximum(live, 1.0)
     row = lax.broadcasted_iota(jnp.int32, (trials, width), 0)
@@ -251,8 +256,9 @@
     rel, base, reach = pl.pallas_call(
         prep_kernel,
         name="prep",
+        compiler_params=pltpu.CompilerParams(vmem_limit_bytes=GRANT),
         out_shape=(
-            jax.ShapeDtypeStruct((trials, NCHAN), f32),
+            jax.ShapeDtypeStruct((trials, NCHAN), bf16),
             jax.ShapeDtypeStruct((NTILE, trials, LANES), jnp.int32),
             jax.ShapeDtypeStruct((NTILE,), jnp.int32),
         ),
@@ -263,7 +269,8 @@
     partial = pl.pallas_call(
         main_kernel,
         name="channelize",
-        out_shape=jax.ShapeDtypeStruct((trials, window), f32),
+        compiler_params=pltpu.CompilerParams(vmem_limit_bytes=GRANT),
+        out_shape=jax.ShapeDtypeStruct((count, trials, window), f32),
         in_specs=[smem] + [vmem] * 8,
         out_specs=vmem,
         scratch_shapes=[
@@ -274,18 +281,20 @@
             pltpu.VMEM((NTILE, trials, window), f32),
         ],
     )(reach, framed, hist, coeffs, first, twist, second, rel, base)
-    parts = lax.all_to_all(jnp.broadcast_to(partial[None], (count, trials, window)), "tm", 0, 0)
+    parts = lax.all_to_all(partial, "tm", 0, 0)
     here = lax.axis_index("tm").astype(jnp.int32).reshape(1)
-    return pl.pallas_call(
+    zscore, trial_stats = pl.pallas_call(
         stats_kernel,
         name="normalize",
+        compiler_params=pltpu.CompilerParams(vmem_limit_bytes=GRANT),
         out_shape=(
-            jax.ShapeDtypeStruct((trials, frames), f32),
+            jax.ShapeDtypeStruct((frames, trials), f32),
             jax.ShapeDtypeStruct((3, trials), f32),
         ),
         in_specs=[smem, vmem, vmem],
         out_specs=(vmem, vmem),
     )(here, parts, mask_row)
+    return zscore.T, trial_stats
 
 
 def solution(mesh):

time: 47.5 us -> 40.6 us (0.85)
  local copies, waits for them, and re-layouts: 5.91 us -> 1.5 us
  Pallas kernels: 13.6 us -> 10.1 us
  starting transfers between devices: 12.5 us -> 13.7 us
    pallas_call x3, Pallas kernels: 13.6 us -> 10.1 us  [the longest x1 7.78 us: per_device(): pl.pallas_call(main_kernel, name='channelize', compiler_params=pltpu.Comp...]
    broadcast_in_dim x1 -> x0, local copies, waits for them, and re-layouts: 1.6 us -> none  [per_device(): jnp.broadcast_to(partial[None], (count, trials, window))]
    pallas_call x1 -> x0, local copies, waits for them, and re-layouts: 1.44 us -> none  [per_device(): pl.pallas_call(stats_kernel, name='normalize', out_shape=(jax.ShapeDtypeS...]
    unnamed x6 -> x14, local copies, waits for them, and re-layouts: 1.47 us -> 0.04 us
    all_to_all x1, starting transfers between devices: 10.1 us -> 11.2 us  [per_device(): parts = lax.all_to_all(partial, 'tm', 0, 0)]
  transfers between devices with their start and end apart: 2 -> 2, of which waited for: 1 -> 1; matrix products, arithmetic and copies ran while one was open for 0% -> 0% of each run, Pallas kernels for 5% -> 3%
where the time goes in v3:
time: 40.6 us; the launch traced here: 40.3 us
  waiting for transfers between devices  14.3 us (35%)
  starting transfers between devices  13.7 us (34%)
  Pallas kernels  10.1 us (25%)
  local copies, waits for them, and re-layouts  1.5 us (4%)
  between operations  0.79 us (2%)
    all_to_all x1, waiting for transfers between devices, per_device(): parts = lax.all_to_all(partial, 'tm', 0, 0)  14.3 us
    all_to_all x1, starting transfers between devices, per_device(): parts = lax.all_to_all(partial, 'tm', 0, 0)  11.2 us
    pallas_call x1, Pallas kernels, per_device(): pl.pallas_call(main_kernel, name='channelize', compiler_params=pltpu.Comp...  7.78 us
    ppermute x1, starting transfers between devices, per_device(): lax.ppermute(framed[:, (frames - TAPS + 1) * RADIX:], 'tm', [(i, i + 1) f...  2.54 us
    reshape x1, local copies, waits for them, and re-layouts, per_device(): framed = voltage.reshape(4, frames * RADIX, LANES)  1.44 us
    pallas_call x1, Pallas kernels, per_device(): pl.pallas_call(prep_kernel, name='prep', compiler_params=pltpu.CompilerPa...  1.24 us
    pallas_call x1, Pallas kernels, per_device(): pl.pallas_call(stats_kernel, name='normalize', compiler_params=pltpu.Comp...  1.04 us
  transfers between devices with their start and end apart: 2, of which 1 were waited for; matrix products, arithmetic and copies ran while one was open for 0% of the time, Pallas kernels for 3%

profile of v3, /device:TPU:0, one launch (start us, length us, event | category | flops | bytes accessed | tf_op | source)
XLA Modules:
  0.0 40.3 jit_solution(8180169917903624050)
XLA Ops:
  0.6 0.0 copy-start
  0.6 1.4 %reshape.15.x_ref = bf16[4,512,128]{2,1,0:T(8,128)(2,1)S(1)} reshape(bf16[2,2,65536]{2,1,0:T(2,128)(2,1)} %param.8) | data formatting | bytes 1048576 | tf_op jit(solution)/shard_map/reshape | solution.py:248
  2.1 0.0 copy-start.5
  2.1 0.0 copy-start.6
  2.1 0.0 copy-start.4
  2.1 2.5 %collective-permute-start = (bf16[4,240,128]{2,1,0:T(8,128)(2,1)S(1)}, bf16[4,240,128]{2,1,0:T(8,128)(2,1)S(1)}, u32[]{:S(2)}, u32[]{:S(2)}) collective-permute-start(bf16[4,240,128]{2,1,0:T(8,128)(2,1)S(1)} %slice.4), channel_id=1, source_target_pairs={{0,1},{1,2},{2,3},{3,4},{4,5},{5,6},{6,7},{7,8},{8,9},{9,10},{10,1... | collective-permute-start | bytes 737288 | tf_op jit(solution)/shard_map/ppermute | solution.py:250
  4.7 0.0 copy-done
  4.7 0.0 copy-done.5
  4.7 0.0 copy-done.6
  4.7 0.0 copy-start.1
  4.7 0.0 copy-start.2
  4.8 0.0 copy-start.3
  4.8 1.2 %prep.1 = (bf16[64,2048]{1,0:T(8,128)(2,1)S(1)}, s32[8,64,128]{2,1,0:T(8,128)S(1)}, s32[8]{0:T(128)S(1)}) custom-call(s32[64,2048]{1,0:T(8,128)S(1)} %copy-done, s32[1,2048]{1,0:T(1,128)S(1)} %bitcast.3, bf16[256,256]{1,0:T(8,128)(2,1)S(1)} %copy-done.5), custom_call_target="tpu_custom_call" | custom-call | tf_op jit(solution)/shard_map/prep/pallas_call | solution.py:256
  6.0 0.0 collective-permute-done.hist_ref
  6.0 0.0 copy-done.4
  6.0 0.0 copy-done.1
  6.0 0.0 copy-done.2
  6.1 0.0 copy-done.3
  6.1 7.8 %channelize.1 = f32[16,64,128]{2,1,0:T(8,128)} custom-call(s32[8]{0:T(128)S(1)} %get-tuple-element.7.reach_ref, bf16[4,512,128]{2,1,0:T(8,128)(2,1)S(1)} %reshape.15.x_ref, bf16[4,240,128]{2,1,0:T(8,128)(2,1)S(1)} %collective-permute-done.hist_ref, f32[256,128]{1,0:T(8,128)S(1)} %copy-done.3, bf16[2,256,256]{2,1,0:T(8,128)(2,1)S(1)} %copy-done.1, ...), custom_call_target="tpu_custom_call" | custom-call | tf_op jit(solution)/shard_map/channelize/pallas_call | solution.py:269
  13.8 11.2 %all-to-all-start = ((f32[16,64,128]{2,1,0:T(8,128)}), f32[16,64,128]{2,1,0:T(8,128)S(1)}, u32[]{:S(2)}, u32[]{:S(2)}) async-start(f32[16,64,128]{2,1,0:T(8,128)} %channelize.1), calls=%async_computation | async-start | bytes 1048576 | tf_op jit(solution)/shard_map/all_to_all | solution.py:284
  25.0 14.3 %all-to-all-done.parts_ref = f32[16,64,128]{2,1,0:T(8,128)S(1)} async-done(((f32[16,64,128]{2,1,0:T(8,128)}), f32[16,64,128]{2,1,0:T(8,128)S(1)}, u32[]{:S(2)}, u32[]{:S(2)}) %all-to-all-start) | async-done | bytes 524320 | tf_op jit(solution)/shard_map/all_to_all | solution.py:284
  39.3 1.0 %normalize.1 = (f32[32,64]{1,0:T(8,128)}, f32[3,64]{1,0:T(4,128)}) custom-call(s32[1]{0:T(128)} %bitcast.where_ref, f32[16,64,128]{2,1,0:T(8,128)S(1)} %all-to-all-done.parts_ref, s32[1,2048]{1,0:T(1,128)S(1)} %bitcast.4), custom_call_target="tpu_custom_call" | custom-call | tf_op jit(solution)/shard_map/normalize/pallas_call | solution.py:286
  (1 shorter events, 0.0 us)
Async XLA Ops:
  0.6 4.1 %copy-start = (s32[64,2048]{1,0:T(8,128)S(1)}, s32[64,2048]{1,0:T(8,128)}, u32[]{:S(2)}) copy-start(s32[64,2048]{1,0:T(8,128)} %delays_ref.1) | copy-start | bytes 1572868
  2.1 2.6 %copy-start.5 = (bf16[256,256]{1,0:T(8,128)(2,1)S(1)}, bf16[256,256]{1,0:T(8,128)(2,1)}, u32[]{:S(2)}) copy-start(bf16[256,256]{1,0:T(8,128)(2,1)} %constant.14.clone.order_ref) | copy-start | bytes 393220
  2.1 2.6 %copy-start.6 = (s32[2048]{0:T(1024)S(1)}, s32[2048]{0:T(1024)}, u32[]{:S(2)}) copy-start(s32[2048]{0:T(1024)} %param.10) | copy-start | bytes 24580
  2.1 3.9 %copy-start.4 = (f32[2,128,128]{2,1,0:T(8,128)S(1)}, f32[2,128,128]{2,1,0:T(8,128)}, u32[]{:S(2)}) copy-start(f32[2,128,128]{2,1,0:T(8,128)} %constant.17.clone.twist_ref) | copy-start | bytes 393220
  2.1 3.9 %collective-permute-start = (bf16[4,240,128]{2,1,0:T(8,128)(2,1)S(1)}, bf16[4,240,128]{2,1,0:T(8,128)(2,1)S(1)}, u32[]{:S(2)}, u32[]{:S(2)}) collective-permute-start(bf16[4,240,128]{2,1,0:T(8,128)(2,1)S(1)} %slice.4), channel_id=1, source_target_pairs={{0,1},{1,2},{2,3},{3,4},{4,5},{5,6},{6,7},{7,8},{8,9},{9,10},{10,1... | collective-permute-start | bytes 737288 | tf_op jit(solution)/shard_map/ppermute | solution.py:250
  4.7 1.3 %copy-start.1 = (bf16[2,256,256]{2,1,0:T(8,128)(2,1)S(1)}, bf16[2,256,256]{2,1,0:T(8,128)(2,1)}, u32[]{:S(2)}) copy-start(bf16[2,256,256]{2,1,0:T(8,128)(2,1)} %constant.16.clone.first_ref) | copy-start | bytes 786436
  4.7 1.3 %copy-start.2 = (bf16[2,256,256]{2,1,0:T(8,128)(2,1)S(1)}, bf16[2,256,256]{2,1,0:T(8,128)(2,1)}, u32[]{:S(2)}) copy-start(bf16[2,256,256]{2,1,0:T(8,128)(2,1)} %constant.18.clone.second_ref) | copy-start | bytes 786436
  4.8 1.3 %copy-start.3 = (f32[256,128]{1,0:T(8,128)S(1)}, f32[256,128]{1,0:T(8,128)}, u32[]{:S(2)}) copy-start(f32[256,128]{1,0:T(8,128)} %constant.15.clone.coeffs_ref) | copy-start | bytes 393220
  13.8 25.4 %all-to-all-start = ((f32[16,64,128]{2,1,0:T(8,128)}), f32[16,64,128]{2,1,0:T(8,128)S(1)}, u32[]{:S(2)}, u32[]{:S(2)}) async-start(f32[16,64,128]{2,1,0:T(8,128)} %channelize.1), calls=%async_computation | async-start | bytes 1048576 | tf_op jit(solution)/shard_map/all_to_all | solution.py:284

commit v4 on v3

--- a/solution.py
+++ b/solution.py
@@ -71,27 +71,7 @@
     return pltpu.roll(value, (width - steps) % width, axis=value.ndim - 1)
 
 
-def prep_kernel(delays_ref, mask_ref, order_ref, rel_ref, base_ref, reach_ref):
-    order = order_ref[...]
-    for tile in range(NTILE):
-        here = delays_ref[:, tile * TILE : (tile + 1) * TILE]
-        least = here[:, TILE - 1 : TILE]
-        live = mask_ref[:, tile * TILE : (tile + 1) * TILE] > 0
-        rel = jnp.where(live, here - least, -1).astype(f32).astype(bf16)
-        rel_ref[:, tile * TILE : (tile + 1) * TILE] = dot(rel, order).astype(bf16)
-        base_ref[tile] = jnp.broadcast_to(least, base_ref.shape[1:])
-        reach_ref[tile] = jnp.max(here[:, 0:1] - least)
-
-
-def main_kernel(reach_ref, x_ref, hist_ref, coeffs_ref, first_ref, twist_ref, second_ref, rel_ref,
-                base_ref, out_ref, ext_ref, weighted_ref, det_ref, tile_ref, acc_ref):
-    frames = x_ref.shape[1] // RADIX
-    past = (TAPS - 1) * RADIX
-    for plane in range(4):
-        ext_ref[plane, :past] = hist_ref[plane].astype(f32)
-        ext_ref[plane, past:] = x_ref[plane].astype(f32)
-    tile_ref[...] = jnp.zeros_like(tile_ref)
-
+def detect(ext_ref, coeffs_ref, first_ref, twist_ref, second_ref, weighted_ref, det_ref):
     for half in range(RADIX // 8):
         taps = [coeffs_ref[tap * RADIX + half * 8 : tap * RADIX + half * 8 + 8] for tap in range(TAPS)]
 
@@ -108,11 +88,11 @@
                     weighted_ref[group, row : row + 8, pol * LANES : (pol + 1) * LANES] = total
             return carry
 
-        lax.fori_loop(0, frames // GROUP, weigh, 0)
+        lax.fori_loop(0, det_ref.shape[0] // (GROUP * RADIX), weigh, 0)
 
     span = GROUP * RADIX
     twist_cos, twist_sin = twist_ref[0], twist_ref[1]
-    for group in range(frames // GROUP):
+    for group in range(det_ref.shape[0] // (GROUP * RADIX)):
         high, low = halves(weighted_ref[group])
         mixed = dot(first_ref[0], high) + dot(first_ref[0], low) + dot(first_ref[1], high)
         energy = None
@@ -128,6 +108,37 @@
             power = square[:, :LANES] + square[:, LANES:]
             energy = power if energy is None else energy + power
         det_ref[group * span : (group + 1) * span] = energy.astype(bf16).astype(f32)
+
+
+def early_kernel(delays_ref, mask_ref, order_ref, x_ref, coeffs_ref, first_ref, twist_ref, second_ref,
+                 rel_ref, base_ref, reach_ref, late_ref, ext_ref, weighted_ref):
+    start = x_ref.shape[1] - ext_ref.shape[1]
+    for plane in range(4):
+        ext_ref[plane] = x_ref[plane, start:].astype(f32)
+    detect(ext_ref, coeffs_ref, first_ref, twist_ref, second_ref, weighted_ref, late_ref)
+    order = order_ref[...]
+    for tile in range(NTILE):
+        here = delays_ref[:, tile * TILE : (tile + 1) * TILE]
+        least = here[:, TILE - 1 : TILE]
+        live = mask_ref[:, tile * TILE : (tile + 1) * TILE] > 0
+        rel = jnp.where(live, here - least, -1).astype(f32).astype(bf16)
+        rel_ref[:, tile * TILE : (tile + 1) * TILE] = dot(rel, order).astype(bf16)
+        base_ref[tile] = jnp.broadcast_to(least, base_ref.shape[1:])
+        reach_ref[tile] = jnp.max(here[:, 0:1] - least)
+
+
+def main_kernel(reach_ref, x_ref, hist_ref, coeffs_ref, first_ref, twist_ref, second_ref, rel_ref,
+                base_ref, late_ref, out_ref, ext_ref, weighted_ref, first_det_ref, det_ref, tile_ref, acc_ref):
+    frames = x_ref.shape[1] // RADIX
+    past = (TAPS - 1) * RADIX
+    middle = frames // 2 * RADIX
+    for plane in range(4):
+        ext_ref[plane, :past] = hist_ref[plane].astype(f32)
+        ext_ref[plane, past:] = x_ref[plane, :middle].astype(f32)
+    tile_ref[...] = jnp.zeros_like(tile_ref)
+    detect(ext_ref, coeffs_ref, first_ref, twist_ref, second_ref, weighted_ref, first_det_ref)
+    det_ref[:middle] = first_det_ref[...]
+    det_ref[middle:] = late_ref[...]
 
     width = LANES // 8
     lane_group = lax.broadcasted_iota(jnp.int32, (frames, LANES), 1) // width
@@ -253,34 +264,41 @@
     mask_row = chan_mask.reshape(1, NCHAN)
     vmem = pl.BlockSpec(memory_space=pltpu.VMEM)
     smem = pl.BlockSpec(memory_space=pltpu.SMEM)
-    rel, base, reach = pl.pallas_call(
-        prep_kernel,
-        name="prep",
+    half = frames // 2
+    rel, base, reach, late = pl.pallas_call(
+        early_kernel,
+        name="early",
         compiler_params=pltpu.CompilerParams(vmem_limit_bytes=GRANT),
         out_shape=(
             jax.ShapeDtypeStruct((trials, NCHAN), bf16),
             jax.ShapeDtypeStruct((NTILE, trials, LANES), jnp.int32),
             jax.ShapeDtypeStruct((NTILE,), jnp.int32),
+            jax.ShapeDtypeStruct((half * RADIX, LANES), f32),
         ),
-        in_specs=[vmem] * 3,
-        out_specs=(vmem, vmem, smem),
-    )(delays, mask_row, order)
+        in_specs=[vmem] * 8,
+        out_specs=(vmem, vmem, smem, vmem),
+        scratch_shapes=[
+            pltpu.VMEM((4, (half + TAPS - 1) * RADIX, LANES), f32),
+            pltpu.VMEM((half // GROUP, 2 * GROUP * RADIX, 2 * LANES), f32),
+        ],
+    )(delays, mask_row, order, framed, coeffs, first, twist, second)
     window = (DSPAN + 1) * frames
     partial = pl.pallas_call(
         main_kernel,
         name="channelize",
         compiler_params=pltpu.CompilerParams(vmem_limit_bytes=GRANT),
         out_shape=jax.ShapeDtypeStruct((count, trials, window), f32),
-        in_specs=[smem] + [vmem] * 8,
+        in_specs=[smem] + [vmem] * 9,
         out_specs=vmem,
         scratch_shapes=[
-            pltpu.VMEM((4, (frames + TAPS - 1) * RADIX, LANES), f32),
-            pltpu.VMEM((frames // GROUP, 2 * GROUP * RADIX, 2 * LANES), f32),
+            pltpu.VMEM((4, (half + TAPS - 1) * RADIX, LANES), f32),
+            pltpu.VMEM((half // GROUP, 2 * GROUP * RADIX, 2 * LANES), f32),
+            pltpu.VMEM((half * RADIX, LANES), f32),
             pltpu.VMEM((frames * RADIX, LANES), f32),
             pltpu.VMEM((NTILE, window, TILE), bf16),
             pltpu.VMEM((NTILE, trials, window), f32),
         ],
-    )(reach, framed, hist, coeffs, first, twist, second, rel, base)
+    )(reach, framed, hist, coeffs, first, twist, second, rel, base, late)
     parts = lax.all_to_all(partial, "tm", 0, 0)
     here = lax.axis_index("tm").astype(jnp.int32).reshape(1)
     zscore, trial_stats = pl.pallas_call(

time: 40.6 us -> 39.6 us (0.975)
  starting transfers between devices: 13.7 us -> 12.8 us
    pallas_call x1, Pallas kernels: 7.78 us -> 6.7 us  [per_device(): pl.pallas_call(main_kernel, name='channelize', compiler_params=pltpu.Comp...]
    pallas_call x1, Pallas kernels: 1.24 us -> 2.12 us  [per_device(): pl.pallas_call(early_kernel, name='early', compiler_params=pltpu.Compiler...]
    all_to_all x1, starting transfers between devices: 11.2 us -> 10.3 us  [per_device(): parts = lax.all_to_all(partial, 'tm', 0, 0)]
  transfers between devices with their start and end apart: 2 -> 2, of which waited for: 1 -> 1; matrix products, arithmetic and copies ran while one was open for 0% -> 0% of each run, Pallas kernels for 3% -> 5%
where the time goes in v4:
time: 39.6 us; the launch traced here: 39.3 us
  waiting for transfers between devices  14.3 us (36%)
  starting transfers between devices  12.8 us (32%)
  Pallas kernels  9.86 us (25%)
  local copies, waits for them, and re-layouts  1.53 us (4%)
  between operations  0.79 us (2%)
    all_to_all x1, waiting for transfers between devices, per_device(): parts = lax.all_to_all(partial, 'tm', 0, 0)  14.3 us
    all_to_all x1, starting transfers between devices, per_device(): parts = lax.all_to_all(partial, 'tm', 0, 0)  10.3 us
    pallas_call x1, Pallas kernels, per_device(): pl.pallas_call(main_kernel, name='channelize', compiler_params=pltpu.Comp...  6.7 us
    ppermute x1, starting transfers between devices, per_device(): lax.ppermute(framed[:, (frames - TAPS + 1) * RADIX:], 'tm', [(i, i + 1) f...  2.54 us
    pallas_call x1, Pallas kernels, per_device(): pl.pallas_call(early_kernel, name='early', compiler_params=pltpu.Compiler...  2.12 us
    reshape x1, local copies, waits for them, and re-layouts, per_device(): framed = voltage.reshape(4, frames * RADIX, LANES)  1.46 us
    pallas_call x1, Pallas kernels, per_device(): pl.pallas_call(stats_kernel, name='normalize', compiler_params=pltpu.Comp...  1.04 us
  transfers between devices with their start and end apart: 2, of which 1 were waited for; matrix products, arithmetic and copies ran while one was open for 0% of the time, Pallas kernels for 5%

profile of v4, /device:TPU:0, one launch (start us, length us, event | category | flops | bytes accessed | tf_op | source)
XLA Modules:
  0.0 39.3 jit_solution(10882177710162186305)
XLA Ops:
  0.6 0.0 copy-start.1
  0.6 0.0 copy-start.2
  0.7 0.0 copy-start.4
  0.7 0.0 copy-start.5
  0.7 1.5 %reshape.15.x_ref = bf16[4,512,128]{2,1,0:T(8,128)(2,1)S(1)} reshape(bf16[2,2,65536]{2,1,0:T(2,128)(2,1)} %param.8) | data formatting | bytes 1048576 | tf_op jit(solution)/shard_map/reshape | solution.py:259
  2.1 0.0 copy-start
  2.2 0.0 copy-start.3
  2.2 0.0 copy-start.6
  2.2 2.5 %collective-permute-start = (bf16[4,240,128]{2,1,0:T(8,128)(2,1)S(1)}, bf16[4,240,128]{2,1,0:T(8,128)(2,1)S(1)}, u32[]{:S(2)}, u32[]{:S(2)}) collective-permute-start(bf16[4,240,128]{2,1,0:T(8,128)(2,1)S(1)} %slice.4), channel_id=1, source_target_pairs={{0,1},{1,2},{2,3},{3,4},{4,5},{5,6},{6,7},{7,8},{8,9},{9,10},{10,1... | collective-permute-start | bytes 737288 | tf_op jit(solution)/shard_map/ppermute | solution.py:261
  4.8 0.0 copy-done.1
  4.8 0.0 copy-done.2
  4.8 0.0 copy-done.4
  4.8 0.0 copy-done.5
  4.8 0.0 copy-done
  4.8 0.0 copy-done.3
  4.8 0.0 copy-done.6
  4.8 2.1 %early.1 = (bf16[64,2048]{1,0:T(8,128)(2,1)S(1)}, s32[8,64,128]{2,1,0:T(8,128)S(1)}, s32[8]{0:T(128)S(1)}, f32[256,128]{1,0:T(8,128)S(1)}) custom-call(s32[64,2048]{1,0:T(8,128)S(1)} %copy-done.2, s32[1,2048]{1,0:T(1,128)S(1)} %bitcast.3, bf16[256,256]{1,0:T(8,128)(2,1)S(1)} %copy-done.5, bf16[4,512,128]{2,1,0:T(8,128)(2,1)S(1)} %reshape.15.x_ref, ...), custom_call_target="tpu_custom_call" | custom-call | tf_op jit(solution)/shard_map/early/pallas_call | solution.py:268
  7.0 0.0 collective-permute-done.hist_ref
  7.0 6.7 %channelize.1 = f32[16,64,128]{2,1,0:T(8,128)} custom-call(s32[8]{0:T(128)S(1)} %get-tuple-element.8.reach_ref, bf16[4,512,128]{2,1,0:T(8,128)(2,1)S(1)} %reshape.15.x_ref, bf16[4,240,128]{2,1,0:T(8,128)(2,1)S(1)} %collective-permute-done.hist_ref, f32[256,128]{1,0:T(8,128)S(1)} %copy-done.3, bf16[2,256,256]{2,1,0:T(8,128)(2,1)S(1)} %copy-done, ...), custom_call_target="tpu_custom_call" | custom-call | tf_op jit(solution)/shard_map/channelize/pallas_call | solution.py:286
  13.7 10.3 %all-to-all-start = ((f32[16,64,128]{2,1,0:T(8,128)}), f32[16,64,128]{2,1,0:T(8,128)S(1)}, u32[]{:S(2)}, u32[]{:S(2)}) async-start(f32[16,64,128]{2,1,0:T(8,128)} %channelize.1), calls=%async_computation | async-start | bytes 1048576 | tf_op jit(solution)/shard_map/all_to_all | solution.py:302
  24.0 14.3 %all-to-all-done.parts_ref = f32[16,64,128]{2,1,0:T(8,128)S(1)} async-done(((f32[16,64,128]{2,1,0:T(8,128)}), f32[16,64,128]{2,1,0:T(8,128)S(1)}, u32[]{:S(2)}, u32[]{:S(2)}) %all-to-all-start) | async-done | bytes 524320 | tf_op jit(solution)/shard_map/all_to_all | solution.py:302
  38.2 1.0 %normalize.1 = (f32[32,64]{1,0:T(8,128)}, f32[3,64]{1,0:T(4,128)}) custom-call(s32[1]{0:T(128)} %bitcast.where_ref, f32[16,64,128]{2,1,0:T(8,128)S(1)} %all-to-all-done.parts_ref, s32[1,2048]{1,0:T(1,128)S(1)} %bitcast.4), custom_call_target="tpu_custom_call" | custom-call | tf_op jit(solution)/shard_map/normalize/pallas_call | solution.py:304
  (1 shorter events, 0.0 us)
Async XLA Ops:
  0.6 4.1 %copy-start.1 = (bf16[2,256,256]{2,1,0:T(8,128)(2,1)S(1)}, bf16[2,256,256]{2,1,0:T(8,128)(2,1)}, u32[]{:S(2)}) copy-start(bf16[2,256,256]{2,1,0:T(8,128)(2,1)} %constant.18.clone.second_ref) | copy-start | bytes 786436
  0.6 4.1 %copy-start.2 = (s32[64,2048]{1,0:T(8,128)S(1)}, s32[64,2048]{1,0:T(8,128)}, u32[]{:S(2)}) copy-start(s32[64,2048]{1,0:T(8,128)} %delays_ref.1) | copy-start | bytes 1572868
  0.7 4.1 %copy-start.4 = (f32[2,128,128]{2,1,0:T(8,128)S(1)}, f32[2,128,128]{2,1,0:T(8,128)}, u32[]{:S(2)}) copy-start(f32[2,128,128]{2,1,0:T(8,128)} %constant.17.clone.twist_ref) | copy-start | bytes 393220
  0.7 4.1 %copy-start.5 = (bf16[256,256]{1,0:T(8,128)(2,1)S(1)}, bf16[256,256]{1,0:T(8,128)(2,1)}, u32[]{:S(2)}) copy-start(bf16[256,256]{1,0:T(8,128)(2,1)} %constant.14.clone.order_ref) | copy-start | bytes 393220
  2.1 2.7 %copy-start = (bf16[2,256,256]{2,1,0:T(8,128)(2,1)S(1)}, bf16[2,256,256]{2,1,0:T(8,128)(2,1)}, u32[]{:S(2)}) copy-start(bf16[2,256,256]{2,1,0:T(8,128)(2,1)} %constant.16.clone.first_ref) | copy-start | bytes 786436
  2.2 2.7 %copy-start.3 = (f32[256,128]{1,0:T(8,128)S(1)}, f32[256,128]{1,0:T(8,128)}, u32[]{:S(2)}) copy-start(f32[256,128]{1,0:T(8,128)} %constant.15.clone.coeffs_ref) | copy-start | bytes 393220
  2.2 2.7 %copy-start.6 = (s32[2048]{0:T(1024)S(1)}, s32[2048]{0:T(1024)}, u32[]{:S(2)}) copy-start(s32[2048]{0:T(1024)} %param.10) | copy-start | bytes 24580
  2.2 4.7 %collective-permute-start = (bf16[4,240,128]{2,1,0:T(8,128)(2,1)S(1)}, bf16[4,240,128]{2,1,0:T(8,128)(2,1)S(1)}, u32[]{:S(2)}, u32[]{:S(2)}) collective-permute-start(bf16[4,240,128]{2,1,0:T(8,128)(2,1)S(1)} %slice.4), channel_id=1, source_target_pairs={{0,1},{1,2},{2,3},{3,4},{4,5},{5,6},{6,7},{7,8},{8,9},{9,10},{10,1... | collective-permute-start | bytes 737288 | tf_op jit(solution)/shard_map/ppermute | solution.py:261
  13.7 24.6 %all-to-all-start = ((f32[16,64,128]{2,1,0:T(8,128)}), f32[16,64,128]{2,1,0:T(8,128)S(1)}, u32[]{:S(2)}, u32[]{:S(2)}) async-start(f32[16,64,128]{2,1,0:T(8,128)} %channelize.1), calls=%async_computation | async-start | bytes 1048576 | tf_op jit(solution)/shard_map/all_to_all | solution.py:302

commit v5 on v4

--- a/solution.py
+++ b/solution.py
@@ -178,9 +178,9 @@
             sums = lax.dot_general(
                 chosen, tile_ref[tile], (((1,), (1,)), ((), ())), preferred_element_type=f32
             )
-            acc = acc_ref[tile]
-            for offset in reversed(range(CHUNK)):
-                acc = roll_left(acc, 1) + sums[offset * trials : (offset + 1) * trials]
+            acc = roll_left(acc_ref[tile], CHUNK) + sums[:trials]
+            for offset in range(1, CHUNK):
+                acc = acc + roll_left(sums[offset * trials : (offset + 1) * trials], offset)
             acc_ref[tile] = acc
         return carry
 

time: 39.6 us -> 38.7 us (0.977)
  Pallas kernels: 9.86 us -> 8.98 us
    pallas_call x1, Pallas kernels: 6.7 us -> 5.82 us  [per_device(): pl.pallas_call(main_kernel, name='channelize', compiler_params=pltpu.Comp...]
  transfers between devices with their start and end apart: 2 -> 2, of which waited for: 1 -> 1; matrix products, arithmetic and copies ran while one was open for 0% -> 0% of each run, Pallas kernels for 5% -> 6%
where the time goes in v5:
time: 38.7 us; the launch traced here: 38.4 us
  waiting for transfers between devices  14.3 us (37%)
  starting transfers between devices  12.8 us (33%)
  Pallas kernels  8.98 us (23%)
  local copies, waits for them, and re-layouts  1.53 us (4%)
  between operations  0.79 us (2%)
    all_to_all x1, waiting for transfers between devices, per_device(): parts = lax.all_to_all(partial, 'tm', 0, 0)  14.3 us
    all_to_all x1, starting transfers between devices, per_device(): parts = lax.all_to_all(partial, 'tm', 0, 0)  10.3 us
    pallas_call x1, Pallas kernels, per_device(): pl.pallas_call(main_kernel, name='channelize', compiler_params=pltpu.Comp...  5.82 us
    ppermute x1, starting transfers between devices, per_device(): lax.ppermute(framed[:, (frames - TAPS + 1) * RADIX:], 'tm', [(i, i + 1) f...  2.54 us
    pallas_call x1, Pallas kernels, per_device(): pl.pallas_call(early_kernel, name='early', compiler_params=pltpu.Compiler...  2.12 us
    reshape x1, local copies, waits for them, and re-layouts, per_device(): framed = voltage.reshape(4, frames * RADIX, LANES)  1.46 us
    pallas_call x1, Pallas kernels, per_device(): pl.pallas_call(stats_kernel, name='normalize', compiler_params=pltpu.Comp...  1.04 us
  transfers between devices with their start and end apart: 2, of which 1 were waited for; matrix products, arithmetic and copies ran while one was open for 0% of the time, Pallas kernels for 6%

profile of v5, /device:TPU:0, one launch (start us, length us, event | category | flops | bytes accessed | tf_op | source)
XLA Modules:
  0.0 38.4 jit_solution(12500349977186748526)
XLA Ops:
  0.6 0.0 copy-start.1
  0.6 0.0 copy-start.2
  0.7 0.0 copy-start.4
  0.7 0.0 copy-start.5
  0.7 1.5 %reshape.15.x_ref = bf16[4,512,128]{2,1,0:T(8,128)(2,1)S(1)} reshape(bf16[2,2,65536]{2,1,0:T(2,128)(2,1)} %param.8) | data formatting | bytes 1048576 | tf_op jit(solution)/shard_map/reshape | solution.py:259
  2.1 0.0 copy-start
  2.2 0.0 copy-start.3
  2.2 0.0 copy-start.6
  2.2 2.5 %collective-permute-start = (bf16[4,240,128]{2,1,0:T(8,128)(2,1)S(1)}, bf16[4,240,128]{2,1,0:T(8,128)(2,1)S(1)}, u32[]{:S(2)}, u32[]{:S(2)}) collective-permute-start(bf16[4,240,128]{2,1,0:T(8,128)(2,1)S(1)} %slice.4), channel_id=1, source_target_pairs={{0,1},{1,2},{2,3},{3,4},{4,5},{5,6},{6,7},{7,8},{8,9},{9,10},{10,1... | collective-permute-start | bytes 737288 | tf_op jit(solution)/shard_map/ppermute | solution.py:261
  4.8 0.0 copy-done.1
  4.8 0.0 copy-done.2
  4.8 0.0 copy-done.4
  4.8 0.0 copy-done.5
  4.8 0.0 copy-done
  4.8 0.0 copy-done.3
  4.8 0.0 copy-done.6
  4.8 2.1 %early.1 = (bf16[64,2048]{1,0:T(8,128)(2,1)S(1)}, s32[8,64,128]{2,1,0:T(8,128)S(1)}, s32[8]{0:T(128)S(1)}, f32[256,128]{1,0:T(8,128)S(1)}) custom-call(s32[64,2048]{1,0:T(8,128)S(1)} %copy-done.2, s32[1,2048]{1,0:T(1,128)S(1)} %bitcast.3, bf16[256,256]{1,0:T(8,128)(2,1)S(1)} %copy-done.5, bf16[4,512,128]{2,1,0:T(8,128)(2,1)S(1)} %reshape.15.x_ref, ...), custom_call_target="tpu_custom_call" | custom-call | tf_op jit(solution)/shard_map/early/pallas_call | solution.py:268
  7.0 0.0 collective-permute-done.hist_ref
  7.0 5.8 %channelize.1 = f32[16,64,128]{2,1,0:T(8,128)} custom-call(s32[8]{0:T(128)S(1)} %get-tuple-element.8.reach_ref, bf16[4,512,128]{2,1,0:T(8,128)(2,1)S(1)} %reshape.15.x_ref, bf16[4,240,128]{2,1,0:T(8,128)(2,1)S(1)} %collective-permute-done.hist_ref, f32[256,128]{1,0:T(8,128)S(1)} %copy-done.3, bf16[2,256,256]{2,1,0:T(8,128)(2,1)S(1)} %copy-done, ...), custom_call_target="tpu_custom_call" | custom-call | tf_op jit(solution)/shard_map/channelize/pallas_call | solution.py:286
  12.8 10.3 %all-to-all-start = ((f32[16,64,128]{2,1,0:T(8,128)}), f32[16,64,128]{2,1,0:T(8,128)S(1)}, u32[]{:S(2)}, u32[]{:S(2)}) async-start(f32[16,64,128]{2,1,0:T(8,128)} %channelize.1), calls=%async_computation | async-start | bytes 1048576 | tf_op jit(solution)/shard_map/all_to_all | solution.py:302
  23.1 14.3 %all-to-all-done.parts_ref = f32[16,64,128]{2,1,0:T(8,128)S(1)} async-done(((f32[16,64,128]{2,1,0:T(8,128)}), f32[16,64,128]{2,1,0:T(8,128)S(1)}, u32[]{:S(2)}, u32[]{:S(2)}) %all-to-all-start) | async-done | bytes 524320 | tf_op jit(solution)/shard_map/all_to_all | solution.py:302
  37.4 1.0 %normalize.1 = (f32[32,64]{1,0:T(8,128)}, f32[3,64]{1,0:T(4,128)}) custom-call(s32[1]{0:T(128)} %bitcast.where_ref, f32[16,64,128]{2,1,0:T(8,128)S(1)} %all-to-all-done.parts_ref, s32[1,2048]{1,0:T(1,128)S(1)} %bitcast.4), custom_call_target="tpu_custom_call" | custom-call | tf_op jit(solution)/shard_map/normalize/pallas_call | solution.py:304
  (1 shorter events, 0.0 us)
Async XLA Ops:
  0.6 4.1 %copy-start.1 = (bf16[2,256,256]{2,1,0:T(8,128)(2,1)S(1)}, bf16[2,256,256]{2,1,0:T(8,128)(2,1)}, u32[]{:S(2)}) copy-start(bf16[2,256,256]{2,1,0:T(8,128)(2,1)} %constant.18.clone.second_ref) | copy-start | bytes 786436
  0.6 4.1 %copy-start.2 = (s32[64,2048]{1,0:T(8,128)S(1)}, s32[64,2048]{1,0:T(8,128)}, u32[]{:S(2)}) copy-start(s32[64,2048]{1,0:T(8,128)} %delays_ref.1) | copy-start | bytes 1572868
  0.7 4.1 %copy-start.4 = (f32[2,128,128]{2,1,0:T(8,128)S(1)}, f32[2,128,128]{2,1,0:T(8,128)}, u32[]{:S(2)}) copy-start(f32[2,128,128]{2,1,0:T(8,128)} %constant.17.clone.twist_ref) | copy-start | bytes 393220
  0.7 4.1 %copy-start.5 = (bf16[256,256]{1,0:T(8,128)(2,1)S(1)}, bf16[256,256]{1,0:T(8,128)(2,1)}, u32[]{:S(2)}) copy-start(bf16[256,256]{1,0:T(8,128)(2,1)} %constant.14.clone.order_ref) | copy-start | bytes 393220
  2.1 2.7 %copy-start = (bf16[2,256,256]{2,1,0:T(8,128)(2,1)S(1)}, bf16[2,256,256]{2,1,0:T(8,128)(2,1)}, u32[]{:S(2)}) copy-start(bf16[2,256,256]{2,1,0:T(8,128)(2,1)} %constant.16.clone.first_ref) | copy-start | bytes 786436
  2.2 2.7 %copy-start.3 = (f32[256,128]{1,0:T(8,128)S(1)}, f32[256,128]{1,0:T(8,128)}, u32[]{:S(2)}) copy-start(f32[256,128]{1,0:T(8,128)} %constant.15.clone.coeffs_ref) | copy-start | bytes 393220
  2.2 2.7 %copy-start.6 = (s32[2048]{0:T(1024)S(1)}, s32[2048]{0:T(1024)}, u32[]{:S(2)}) copy-start(s32[2048]{0:T(1024)} %param.10) | copy-start | bytes 24580
  2.2 4.7 %collective-permute-start = (bf16[4,240,128]{2,1,0:T(8,128)(2,1)S(1)}, bf16[4,240,128]{2,1,0:T(8,128)(2,1)S(1)}, u32[]{:S(2)}, u32[]{:S(2)}) collective-permute-start(bf16[4,240,128]{2,1,0:T(8,128)(2,1)S(1)} %slice.4), channel_id=1, source_target_pairs={{0,1},{1,2},{2,3},{3,4},{4,5},{5,6},{6,7},{7,8},{8,9},{9,10},{10,1... | collective-permute-start | bytes 737288 | tf_op jit(solution)/shard_map/ppermute | solution.py:261
  12.8 24.6 %all-to-all-start = ((f32[16,64,128]{2,1,0:T(8,128)}), f32[16,64,128]{2,1,0:T(8,128)S(1)}, u32[]{:S(2)}, u32[]{:S(2)}) async-start(f32[16,64,128]{2,1,0:T(8,128)} %channelize.1), calls=%async_computation | async-start | bytes 1048576 | tf_op jit(solution)/shard_map/all_to_all | solution.py:302
